TPU v7x, 256 devices: a whole 4x4x8 slice. The times are simulated.
256 devices in a mesh: dp: 32 (over z, x), patch: 8 (over y, core).
Axes of the slice: x: 4, y: 4, z: 8, core: 2. Of those that a mesh axis runs over, the one named last changes fastest.
Arguments:
- token_ids: int32 [512], replicated, may hold values from 0 to 31999
- parents: int32 [512], replicated, may hold values from 0 to 3
- embedding: bfloat16 [32000, 1024], P('dp'), may hold values from -6 to 6
- self_gain: bfloat16 [1024], replicated, may hold values from 0.25 to 1.75
- query_weight: bfloat16 [1024, 1024], P(None, 'patch'), may hold values from -0.1875 to 0.1875
- key_weight: bfloat16 [1024, 1024], P(None, 'patch'), may hold values from -0.1875 to 0.1875
- value_weight: bfloat16 [1024, 1024], P(None, 'patch'), may hold values from -0.1875 to 0.1875
- output_weight: bfloat16 [1024, 1024], P('patch'), may hold values from -0.75 to 0.75
- past_keys: bfloat16 [512, 128, 1024], P('dp', None, 'patch'), may hold values from -200 to 200
- past_values: bfloat16 [512, 128, 1024], P('dp', None, 'patch'), may hold values from -6 to 6
- cross_gain: bfloat16 [1024], replicated, may hold values from 0.25 to 1.75
- cross_query: bfloat16 [1024, 1024], replicated, may hold values from -0.1875 to 0.1875
- cross_output: bfloat16 [1024, 1024], replicated, may hold values from -0.75 to 0.75
- image_keys: bfloat16 [32, 16, 256, 1024], P('dp', None, 'patch'), may hold values from -260 to 260
- image_values: bfloat16 [32, 16, 256, 1024], P('dp', None, 'patch'), may hold values from -6 to 6
Outputs:
- hidden: bfloat16 [512, 1024], P('dp')
- new_keys: bfloat16 [512, 1024], P('dp', 'patch')
- new_values: bfloat16 [512, 1024], P('dp', 'patch')
Inputs may be any that keep to these rules, and one draw needn't show every extreme that they name: `parents`: a beam of the row's own image.
All inputs are finite; a program needn't handle non-finite values.
Results may differ from a plain program's by a relative error of at most 0.019.
The roundings to bfloat16 on the way count: a program that leaves them out, or rounds other values in their place, can miss the bound.
Values may be sent and summed in bfloat16 or wider, within the bound.
A program may use at most 64 MiB of HBM per device.

v0:
```python
import math

import jax
import jax.numpy as jnp
from jax import lax
from jax.sharding import Mesh
from jax.sharding import PartitionSpec as P

D = 1024
HEADS = 16
BEAMS = 4
PATCH = ("patch_0", "patch_1")


def from_partner(value, axis, distance):
    mask = 2**distance
    pairs = [(source, source ^ mask) for source in range(lax.axis_size(axis))]
    return lax.ppermute(value, axis, pairs)


def combined_by_axis(x, axes, combine):
    for axis in axes:
        pieces = jax.tree.map(lambda part: lax.all_gather(part, axis), x)
        x = jax.tree.map(lambda part: part[0], pieces)
        for k in range(1, lax.axis_size(axis)):
            x = combine(x, jax.tree.map(lambda part: part[k], pieces))
    return x


def copy_for_each(x, axis):
    copies = jnp.broadcast_to(x, (lax.axis_size(axis), *x.shape))
    return lax.all_to_all(copies, axis, split_axis=0, concat_axis=0, tiled=True)


def taken_together(x, axis):
    everything = copy_for_each(x, axis)
    return jnp.sum(everything, axis=0)


def normalize(inputs, gains):
    factor = lax.rsqrt(jnp.mean(inputs * inputs, axis=-1, keepdims=True) + 1e-06)
    return (inputs * factor * gains.astype(jnp.float32)).astype(jnp.bfloat16)


def combine(former, latter):
    peak_former, total_former, sum_former = former
    peak_latter, total_latter, sum_latter = latter
    peaks = jnp.maximum(peak_former, peak_latter)
    former_scale = jnp.exp(peak_former - peaks)
    latter_scale = jnp.exp(peak_latter - peaks)
    heads_count = peaks.shape[-1]
    count_rows = peaks.shape[0]
    sums = (
        sum_former.reshape(count_rows, heads_count, -1) * former_scale[..., None]
        + sum_latter.reshape(count_rows, heads_count, -1) * latter_scale[..., None]
    )
    return (
        peaks,
        total_former * former_scale + total_latter * latter_scale,
        sums.reshape(count_rows, -1),
    )


def beam_collect(pieces, concat_dim):
    for bit_index in range(2):
        partner = from_partner(pieces, "dp", bit_index)
        upper_bit = lax.axis_index("dp") // 2**bit_index % 2
        pieces = jnp.where(
            upper_bit == 1,
            jnp.concatenate([partner, pieces], concat_dim),
            jnp.concatenate([pieces, partner], concat_dim),
        )
    return pieces


def beam_reduce(partial_value):
    for bit_index in (1, 0):
        upper_bit = lax.axis_index("dp") // 2**bit_index % 2
        half_rows = partial_value[0].shape[0] // 2
        keep_part = tuple(
            (
                lax.dynamic_slice_in_dim(member, upper_bit * half_rows, half_rows, 0)
                for member in partial_value
            )
        )
        send_part = tuple(
            (
                lax.dynamic_slice_in_dim(member, (1 - upper_bit) * half_rows, half_rows, 0)
                for member in partial_value
            )
        )
        received = from_partner(send_part, "dp", bit_index)
        partial_value = combine(keep_part, received)
    return partial_value


def patch_merge(partial_value):
    return combined_by_axis(partial_value, PATCH, combine)


def shards(
    token_ids,
    parents,
    embedding,
    self_gain,
    query_weight,
    key_weight,
    value_weight,
    output_weight,
    past_keys,
    past_values,
    cross_gain,
    cross_query,
    cross_output,
    image_keys,
    image_values,
):
    row_count = past_keys.shape[0]
    length = past_keys.shape[1]
    width_here = query_weight.shape[1]
    head_size = D // HEADS
    heads_here = width_here // head_size
    scaling = 1.0 / math.sqrt(head_size)
    position = lax.axis_index("dp")
    slab = embedding.shape[0]
    vocab_ids = position * slab + jnp.arange(slab, dtype=jnp.int32)
    group_count = lax.axis_size("dp")
    onehot_table = (token_ids[:, None] == vocab_ids[None, :]).astype(jnp.bfloat16)
    owned = (
        jnp.dot(onehot_table, embedding, preferred_element_type=jnp.float32)
        .astype(jnp.bfloat16)
        .reshape(group_count, row_count, D)
    )
    arrived = lax.all_to_all(owned, "dp", split_axis=0, concat_axis=0, tiled=True)
    tokens = jnp.sum(arrived.astype(jnp.float32), axis=0)
    normed = normalize(tokens, self_gain)
    queries = jnp.dot(normed, query_weight, preferred_element_type=jnp.float32).astype(jnp.bfloat16)
    new_key = jnp.dot(normed, key_weight, preferred_element_type=jnp.float32).astype(jnp.bfloat16)
    new_value = jnp.dot(normed, value_weight, preferred_element_type=jnp.float32).astype(
        jnp.bfloat16
    )
    query_heads = queries.reshape(row_count, heads_here, head_size)
    key_heads = new_key.reshape(row_count, heads_here, head_size)
    value_heads = new_value.reshape(row_count, heads_here, head_size)
    own_score = (
        jnp.sum(query_heads.astype(jnp.float32) * key_heads.astype(jnp.float32), axis=-1) * scaling
    )
    paired = jnp.stack([queries, new_key], 0)
    gathered = beam_collect(paired, 1).reshape(2, BEAMS, row_count, heads_here, head_size)
    gathered_queries = gathered[0]
    gathered_keys = gathered[1]
    own_every = (
        jnp.sum(gathered_queries.astype(jnp.float32) * gathered_keys.astype(jnp.float32), axis=-1)
        * scaling
    )
    block_start = position // BEAMS * BEAMS * row_count
    block_parents = lax.dynamic_slice_in_dim(parents, block_start, BEAMS * row_count, 0).reshape(
        BEAMS, row_count
    )
    living = (block_parents == position % BEAMS).astype(jnp.float32)
    old_keys = past_keys.reshape(row_count, length, heads_here, head_size)
    old_values = past_values.reshape(row_count, length, heads_here, head_size)
    scores = (
        jnp.einsum(
            "bihe,ilhe->bihl", gathered_queries, old_keys, preferred_element_type=jnp.float32
        )
        * scaling
    )
    maxima = jnp.maximum(jnp.max(scores, axis=-1), own_every)
    powers = jnp.exp(scores - maxima[..., None]) * living[:, :, None, None]
    totals = jnp.sum(powers, axis=-1) + jnp.exp(own_every - maxima) * living[:, :, None]
    numerators = jnp.einsum(
        "bihl,ilhe->bihe",
        powers.astype(jnp.bfloat16),
        old_values,
        preferred_element_type=jnp.float32,
    )
    partial_value = (
        jnp.where(living[:, :, None] > 0.5, maxima, -1e30).reshape(BEAMS * row_count, heads_here),
        totals.reshape(BEAMS * row_count, heads_here),
        numerators.reshape(BEAMS * row_count, width_here),
    )
    peaks, sums, weighted = beam_reduce(partial_value)
    own_weight = jnp.exp(own_score - peaks).astype(jnp.bfloat16).astype(jnp.float32)
    weighted = weighted.reshape(row_count, heads_here, head_size) + own_weight[
        ..., None
    ] * value_heads.astype(jnp.float32)
    self_context = weighted / sums[..., None]
    self_context = self_context.reshape(row_count, width_here).astype(jnp.bfloat16)
    middle = tokens + taken_together(
        jnp.dot(self_context, output_weight, preferred_element_type=jnp.float32), PATCH
    )
    probes = jnp.dot(
        normalize(middle, cross_gain), cross_query, preferred_element_type=jnp.float32
    ).astype(jnp.bfloat16)
    every_probe = beam_collect(probes, 0).reshape(BEAMS, row_count, HEADS, head_size)
    patch_count = image_keys.shape[2]
    patch_keys = image_keys.reshape(row_count, patch_count, HEADS, head_size)
    patch_values = image_values.reshape(row_count, patch_count, HEADS, head_size)
    cross_scores = (
        jnp.einsum("bihe,iphe->bihp", every_probe, patch_keys, preferred_element_type=jnp.float32)
        * scaling
    )
    cross_peaks = jnp.max(cross_scores, axis=-1)
    cross_powers = jnp.exp(cross_scores - cross_peaks[..., None])
    cross_totals = jnp.sum(cross_powers, axis=-1)
    cross_sums = jnp.einsum(
        "bihp,iphe->bihe",
        cross_powers.astype(jnp.bfloat16),
        patch_values,
        preferred_element_type=jnp.float32,
    )
    partial_value = (
        cross_peaks.reshape(BEAMS * row_count, HEADS),
        cross_totals.reshape(BEAMS * row_count, HEADS),
        cross_sums.reshape(BEAMS * row_count, D),
    )
    partial_value = patch_merge(beam_reduce(partial_value))
    cross_context = (
        (partial_value[2].reshape(row_count, HEADS, head_size) / partial_value[1][..., None])
        .reshape(row_count, D)
        .astype(jnp.bfloat16)
    )
    hidden = (
        middle + jnp.dot(cross_context, cross_output, preferred_element_type=jnp.float32)
    ).astype(jnp.bfloat16)
    return (hidden, new_key, new_value)


def solution(mesh):
    split = Mesh(mesh.devices.reshape(mesh.shape["dp"], 4, 2), ("dp", "patch_0", "patch_1"))
    in_specs = (
        P(),
        P(),
        P("dp", None),
        P(),
        P(None, PATCH),
        P(None, PATCH),
        P(None, PATCH),
        P(PATCH, None),
        P("dp", None, PATCH),
        P("dp", None, PATCH),
        P(),
        P(),
        P(),
        P("dp", None, PATCH, None),
        P("dp", None, PATCH, None),
    )
    out_specs = (P("dp", None), P("dp", PATCH), P("dp", PATCH))
    return jax.shard_map(
        shards, mesh=split, in_specs=in_specs, out_specs=out_specs, check_vma=False
    )
```

profile of v0, /device:TPU:1, one launch (start us, length us, event | category | flops | bytes accessed | tf_op | source)
XLA Modules:
  0.0 170.5 jit_solution(5895643656568771161)
XLA Ops:
  0.7 4.0 %fusion.6 = bf16[512,1024]{1,0:T(8,128)(2,1)} fusion(bf16[1000,1024]{1,0:T(8,128)(2,1)} %param.17, s32[1000]{0:T(1024)S(1)} %iota_add_fusion, s32[512]{0:T(512)} %param.15), kind=kOutput, calls=%fused_computation.7 | convolution fusion | flops 1049612288 | bytes 3102624 | tf_op jit(solution)/shard_map/dot_general | solution.py:130
  4.7 12.0 %all-to-all-start = ((bf16[32,16,1024]{2,1,0:T(8,128)(2,1)}), bf16[32,16,1024]{2,1,0:T(8,128)(2,1)S(1)}, u32[]{:S(2)}, u32[]{:S(2)}) async-start(bf16[32,16,1024]{2,1,0:T(8,128)(2,1)} %bitcast.204), calls=%async_computation | async-start | bytes 2097152 | tf_op jit(solution)/shard_map/all_to_all | solution.py:134
  16.7 26.1 %all-to-all-done = bf16[32,16,1024]{2,1,0:T(8,128)(2,1)S(1)} async-done(((bf16[32,16,1024]{2,1,0:T(8,128)(2,1)}), bf16[32,16,1024]{2,1,0:T(8,128)(2,1)S(1)}, u32[]{:S(2)}, u32[]{:S(2)}) %all-to-all-start) | async-done | bytes 1048608 | tf_op jit(solution)/shard_map/all_to_all | solution.py:134
  43.4 1.1 convert_multiply_fusion
  44.5 1.9 %collective-permute-start = (bf16[2,16,128]{2,1,0:T(8,128)(2,1)S(1)}, bf16[2,16,128]{2,1,0:T(8,128)(2,1)S(1)}, u32[]{:S(2)}, u32[]{:S(2)}) collective-permute-start(bf16[2,16,128]{2,1,0:T(8,128)(2,1)S(1)} %pad_maximum_fusion), channel_id=1, source_target_pairs={{0,8},{8,0},{16,24},{24,16},{32,40},{40,32},{48,56},{56,48},{64,72... | collective-permute-start | bytes 24584 | tf_op jit(solution)/shard_map/ppermute | solution.py:18
  46.5 0.8 broadcast_compare_fusion
  47.2 1.3 copy.136
  48.7 2.0 %copy.142 = bf16[16,128,128]{1,2,0:T(8,128)(2,1)} copy(bf16[16,128,128]{2,1,0:T(8,128)(2,1)} %param.24) | data formatting | bytes 1048576 | tf_op args[9]
  50.8 2.8 %collective-permute-start.1 = (bf16[2,32,128]{2,1,0:T(8,128)(2,1)S(1)}, bf16[2,32,128]{2,1,0:T(8,128)(2,1)S(1)}, u32[]{:S(2)}, u32[]{:S(2)}) collective-permute-start(bf16[2,32,128]{2,1,0:T(8,128)(2,1)S(1)} %maximum_select_fusion.3), channel_id=1, source_target_pairs={{0,16},{8,24},{16,0},{24,8},{32,48},{40,56},{48,32},{56,40},{64,80... | collective-permute-start | bytes 49160 | tf_op jit(solution)/shard_map/ppermute | solution.py:18
  54.0 1.0 collective-permute-done.1
  55.4 0.3 fusion.83
  56.0 0.2 fusion.41
  56.3 1.5 convolution_bitcast_fusion
  58.2 2.7 %collective-permute-start.2 = (f32[32,2]{0,1:T(2,128)S(1)}, f32[32,2]{0,1:T(2,128)S(1)}, u32[]{:S(2)}, u32[]{:S(2)}) collective-permute-start(f32[32,2]{0,1:T(2,128)S(1)} %constant_dynamic-slice_fusion.14), channel_id=1, source_target_pairs={{0,16},{8,24},{16,0},{24,8},{32,48},{40,56},{48,32},{56,40},{64,80... | collective-permute-start | bytes 776 | tf_op jit(solution)/shard_map/ppermute | solution.py:18
  61.0 0.3 collective-permute-start.6
  61.3 2.7 %collective-permute-start.3 = (f32[32,128]{1,0:T(8,128)S(1)}, f32[32,128]{1,0:T(8,128)S(1)}, u32[]{:S(2)}, u32[]{:S(2)}) collective-permute-start(f32[32,128]{1,0:T(8,128)S(1)} %constant_dynamic-slice_fusion.13), channel_id=1, source_target_pairs={{0,16},{8,24},{16,0},{24,8},{32,48},{40,56},{48,32},{56,40},{64,80... | collective-permute-start | bytes 49160 | tf_op jit(solution)/shard_map/ppermute | solution.py:18
  64.0 1.0 collective-permute-done.6
  65.8 1.4 collective-permute-start.7
  67.4 0.7 collective-permute-done.4
  69.3 0.8 collective-permute-done.5
  70.3 0.8 broadcast_in_dim.16
  71.2 10.9 %all-to-all-start.1 = ((f32[8,16,1024]{2,1,0:T(8,128)}), f32[8,16,1024]{2,1,0:T(8,128)S(1)}, u32[]{:S(2)}, u32[]{:S(2)}) async-start(f32[8,16,1024]{2,1,0:T(8,128)} %broadcast_in_dim.16), calls=%async_computation.1 | async-start | bytes 1048576 | tf_op jit(solution)/shard_map/all_to_all | solution.py:32
  82.1 9.3 %all-to-all-done.1 = f32[8,16,1024]{2,1,0:T(8,128)S(1)} async-done(((f32[8,16,1024]{2,1,0:T(8,128)}), f32[8,16,1024]{2,1,0:T(8,128)S(1)}, u32[]{:S(2)}, u32[]{:S(2)}) %all-to-all-start.1) | async-done | bytes 524320 | tf_op jit(solution)/shard_map/all_to_all | solution.py:32
  91.6 0.4 convolution_convert_fusion
  92.1 0.6 collective-permute-start.8
  92.7 2.1 %collective-permute-done.8 = bf16[16,1024]{1,0:T(8,128)(2,1)S(1)} collective-permute-done((bf16[16,1024]{1,0:T(8,128)(2,1)S(1)}, bf16[16,1024]{1,0:T(8,128)(2,1)S(1)}, u32[]{:S(2)}, u32[]{:S(2)}) %collective-permute-start.8) | collective-permute-done | bytes 32800 | tf_op jit(solution)/shard_map/ppermute | solution.py:18
  94.8 0.8 collective-permute-start.9
  95.7 2.3 %reshape.315 = bf16[16,32,16,64]{3,2,1,0:T(8,128)(2,1)} reshape(bf16[1,16,32,1024]{3,2,1,0:T(8,128)(2,1)S(1)} %copy-done.1) | data formatting | bytes 2097152 | tf_op jit(solution)/shard_map/reshape | solution.py:198
  98.0 4.0 %reshape.316 = bf16[16,32,16,64]{3,2,1,0:T(8,128)(2,1)} reshape(bf16[1,16,32,1024]{3,2,1,0:T(8,128)(2,1)} %param.29) | data formatting | bytes 2097152 | tf_op jit(solution)/shard_map/reshape | solution.py:199
  102.2 2.9 %fusion.84 = (f32[4,16,16]{0,2,1:T(8,128)S(1)}, f32[4,16,16,32]{3,0,2,1:T(4,128)S(1)}) fusion(bf16[16,32,16,64]{3,2,1,0:T(8,128)(2,1)} %reshape.315, bf16[4,16,16,64]{3,2,1,0:T(8,128)(2,1)S(1)} %select_n.136), kind=kOutput, calls=%fused_computation.164 | convolution fusion | flops 4258816 | bytes 1314816 | tf_op jit(solution)/shard_map/bihe,iphe->bihp/dot_general | solution.py:201
  105.1 0.2 copy.157
  105.5 2.4 %collective-permute-start.10 = (f32[32,16]{0,1:T(8,128)S(1)}, f32[32,16]{0,1:T(8,128)S(1)}, u32[]{:S(2)}, u32[]{:S(2)}) collective-permute-start(f32[32,16]{0,1:T(8,128)S(1)} %constant_dynamic-slice_fusion.5), channel_id=1, source_target_pairs={{0,16},{8,24},{16,0},{24,8},{32,48},{40,56},{48,32},{56,40},{64,80... | collective-permute-start | bytes 6152 | tf_op jit(solution)/shard_map/ppermute | solution.py:18
  107.9 0.7 fusion.22
  108.6 0.2 copy.163
  108.9 0.6 collective-permute-start.14
  109.5 2.3 %fusion.9 = f32[4,16,16,64]{3,0,2,1:T(4,128)S(1)} fusion(bf16[16,32,16,64]{3,2,1,0:T(8,128)(2,1)} %reshape.316, f32[4,16,16,32]{3,0,2,1:T(4,128)S(1)} %get-tuple-element.46, f32[4,16,16]{0,2,1:T(8,128)S(1)} %get-tuple-element.45), kind=kOutput, calls=%fused_computation.8 | convolution fusion | flops 4259840 | bytes 1445888 | tf_op jit(solution)/shard_map/bihp,iphe->bihe/dot_general | solution.py:207
  112.0 0.9 collective-permute-done.14
  113.1 0.7 collective-permute-start.12
  113.8 0.8 collective-permute-start.15
  114.7 1.6 collective-permute-start.11
  117.1 9.3 %all-gather.1 = f32[64,16]{1,0:T(8,128)S(1)} all-gather(f32[16,16]{1,0:T(8,128)S(1)} %copy.162), channel_id=3, replica_groups=mesh['dp'=32,'patch_0'=4,'patch_1'=2] {'patch_0'}, dimensions={0}, use_global_device_ids=true | all-gather | bytes 5120 | tf_op jit(solution)/shard_map/all_gather | solution.py:23
  126.5 9.0 %all-gather.2 = f32[64,16]{1,0:T(8,128)S(1)} all-gather(f32[16,16]{1,0:T(8,128)S(1)} %copy.164), channel_id=4, replica_groups=mesh['dp'=32,'patch_0'=4,'patch_1'=2] {'patch_0'}, dimensions={0}, use_global_device_ids=true | all-gather | bytes 5120 | tf_op jit(solution)/shard_map/all_gather | solution.py:23
  135.5 11.6 %all_gather.30 = f32[2,16,16]{2,1,0:T(8,128)S(1)} all-gather(f32[1,16,16]{2,1,0:T(8,128)S(1)} %get-tuple-element.9), channel_id=1, replica_groups=mesh['dp'=32,'patch_0'=4,'patch_1'=2] {'patch_1'}, dimensions={0}, use_global_device_ids=true | all-gather | bytes 3072 | tf_op jit(solution)/shard_map/all_gather | solution.py:23
  147.1 1.8 %all_gather.33 = f32[2,16,16]{2,1,0:T(8,128)S(1)} all-gather(f32[1,16,16]{2,1,0:T(8,128)S(1)} %get-tuple-element.8), channel_id=1, replica_groups=mesh['dp'=32,'patch_0'=4,'patch_1'=2] {'patch_1'}, dimensions={0}, use_global_device_ids=true | all-gather | bytes 3072 | tf_op jit(solution)/shard_map/all_gather | solution.py:23
  149.0 0.9 collective-permute-start.13
  152.3 9.8 %all-gather = f32[64,1024]{1,0:T(8,128)S(1)} all-gather(f32[16,1024]{1,0:T(8,128)S(1)} %multiply_add_fusion.1), channel_id=2, replica_groups=mesh['dp'=32,'patch_0'=4,'patch_1'=2] {'patch_0'}, dimensions={0}, use_global_device_ids=true | all-gather | bytes 327680 | tf_op jit(solution)/shard_map/all_gather | solution.py:23
  162.2 5.7 %all_gather.29 = f32[2,16,1024]{2,1,0:T(8,128)S(1)} all-gather(f32[1,16,1024]{2,1,0:T(8,128)S(1)} %fusion.32), channel_id=1, replica_groups=mesh['dp'=32,'patch_0'=4,'patch_1'=2] {'patch_1'}, dimensions={0}, use_global_device_ids=true | all-gather | bytes 196608 | tf_op jit(solution)/shard_map/all_gather | solution.py:23
  167.9 2.6 %fusion.19 = bf16[16,1024]{1,0:T(8,128)(2,1)} fusion(f32[16,1024]{1,0:T(8,128)S(1)} %get-tuple-element.19, bf16[1024,1024]{1,0:T(8,128)(2,1)} %param.27, f32[16,1024]{1,0:T(8,128)S(1)} %div.62, f32[16,1024]{1,0:T(8,128)S(1)} %mul.484, f32[2,16,1024]{2,1,0:T(8,128)S(1)} %all_gather.29, f32[16,1024]{1,0:T(8,128)S(1)} %mul.481), kind=kOutput, calls=%fused_computation.15 | convolution fusion | flops 33669120 | bytes 2523136 | tf_op jit(solution)/shard_map/dot_general | solution.py:225
  (147 shorter events, 9.2 us)
Async XLA Ops:
  0.6 91.0 %copy-start = (bf16[1024,1024]{1,0:T(8,128)(2,1)S(1)}, bf16[1024,1024]{1,0:T(8,128)(2,1)}, u32[]{:S(2)}) copy-start(bf16[1024,1024]{1,0:T(8,128)(2,1)} %param.26) | copy-start | bytes 6291460
  4.7 12.0 %copy-start.7 = (bf16[1024]{0:T(1024)(128)(2,1)S(1)}, bf16[1024]{0:T(1024)(128)(2,1)}, u32[]{:S(2)}) copy-start(bf16[1024]{0:T(1024)(128)(2,1)} %param.18) | copy-start | bytes 6148
  4.7 38.6 %copy-start.2 = (bf16[1024,128]{1,0:T(8,128)(2,1)S(1)}, bf16[1024,128]{1,0:T(8,128)(2,1)}, u32[]{:S(2)}) copy-start(bf16[1024,128]{1,0:T(8,128)(2,1)} %param.19) | copy-start | bytes 786436
  4.7 38.2 %all-to-all-start = ((bf16[32,16,1024]{2,1,0:T(8,128)(2,1)}), bf16[32,16,1024]{2,1,0:T(8,128)(2,1)S(1)}, u32[]{:S(2)}, u32[]{:S(2)}) async-start(bf16[32,16,1024]{2,1,0:T(8,128)(2,1)} %bitcast.204), calls=%async_computation | async-start | bytes 2097152 | tf_op jit(solution)/shard_map/all_to_all | solution.py:134
  43.0 10.5 %copy-start.3 = (bf16[1024,128]{1,0:T(8,128)(2,1)S(1)}, bf16[1024,128]{1,0:T(8,128)(2,1)}, u32[]{:S(2)}) copy-start(bf16[1024,128]{1,0:T(8,128)(2,1)} %param.21) | copy-start | bytes 786436
  44.5 13.2 %copy-start.5 = (bf16[16,128]{1,0:T(8,128)(2,1)}, bf16[16,128]{1,0:T(8,128)(2,1)S(1)}, u32[]{:S(2)}) copy-start(bf16[16,128]{1,0:T(8,128)(2,1)S(1)} %get-tuple-element.44) | copy-start | bytes 12292
  44.5 6.2 %collective-permute-start = (bf16[2,16,128]{2,1,0:T(8,128)(2,1)S(1)}, bf16[2,16,128]{2,1,0:T(8,128)(2,1)S(1)}, u32[]{:S(2)}, u32[]{:S(2)}) collective-permute-start(bf16[2,16,128]{2,1,0:T(8,128)(2,1)S(1)} %pad_maximum_fusion), channel_id=1, source_target_pairs={{0,8},{8,0},{16,24},{24,16},{32,40},{40,32},{48,56},{56,48},{64,72... | collective-permute-start | bytes 24584 | tf_op jit(solution)/shard_map/ppermute | solution.py:18
  50.7 19.4 %copy-start.4 = (bf16[128,1024]{1,0:T(8,128)(2,1)S(1)}, bf16[128,1024]{1,0:T(8,128)(2,1)}, u32[]{:S(2)}) copy-start(bf16[128,1024]{1,0:T(8,128)(2,1)} %param.22) | copy-start | bytes 786436
  50.8 4.2 %collective-permute-start.1 = (bf16[2,32,128]{2,1,0:T(8,128)(2,1)S(1)}, bf16[2,32,128]{2,1,0:T(8,128)(2,1)S(1)}, u32[]{:S(2)}, u32[]{:S(2)}) collective-permute-start(bf16[2,32,128]{2,1,0:T(8,128)(2,1)S(1)} %maximum_select_fusion.3), channel_id=1, source_target_pairs={{0,16},{8,24},{16,0},{24,8},{32,48},{40,56},{48,32},{56,40},{64,80... | collective-permute-start | bytes 49160 | tf_op jit(solution)/shard_map/ppermute | solution.py:18
  53.7 17.5 %copy-start.6 = (bf16[16,128]{1,0:T(8,128)(2,1)}, bf16[16,128]{1,0:T(8,128)(2,1)S(1)}, u32[]{:S(2)}) copy-start(bf16[16,128]{1,0:T(8,128)(2,1)S(1)} %convolution_convert_fusion.1) | copy-start | bytes 12292
  55.9 26.2 %copy-start.8 = (bf16[1024]{0:T(1024)(128)(2,1)S(1)}, bf16[1024]{0:T(1024)(128)(2,1)}, u32[]{:S(2)}) copy-start(bf16[1024]{0:T(1024)(128)(2,1)} %param.25) | copy-start | bytes 6148
  58.2 5.8 %collective-permute-start.2 = (f32[32,2]{0,1:T(2,128)S(1)}, f32[32,2]{0,1:T(2,128)S(1)}, u32[]{:S(2)}, u32[]{:S(2)}) collective-permute-start(f32[32,2]{0,1:T(2,128)S(1)} %constant_dynamic-slice_fusion.14), channel_id=1, source_target_pairs={{0,16},{8,24},{16,0},{24,8},{32,48},{40,56},{48,32},{56,40},{64,80... | collective-permute-start | bytes 776 | tf_op jit(solution)/shard_map/ppermute | solution.py:18
  61.0 3.9 %collective-permute-start.6 = (f32[32,2]{0,1:T(2,128)S(1)}, f32[32,2]{0,1:T(2,128)S(1)}, u32[]{:S(2)}, u32[]{:S(2)}) collective-permute-start(f32[32,2]{0,1:T(2,128)S(1)} %constant_dynamic-slice_fusion.8), channel_id=1, source_target_pairs={{0,16},{8,24},{16,0},{24,8},{32,48},{40,56},{48,32},{56,40},{64,80... | collective-permute-start | bytes 776 | tf_op jit(solution)/shard_map/ppermute | solution.py:18
  61.3 5.9 %collective-permute-start.3 = (f32[32,128]{1,0:T(8,128)S(1)}, f32[32,128]{1,0:T(8,128)S(1)}, u32[]{:S(2)}, u32[]{:S(2)}) collective-permute-start(f32[32,128]{1,0:T(8,128)S(1)} %constant_dynamic-slice_fusion.13), channel_id=1, source_target_pairs={{0,16},{8,24},{16,0},{24,8},{32,48},{40,56},{48,32},{56,40},{64,80... | collective-permute-start | bytes 49160 | tf_op jit(solution)/shard_map/ppermute | solution.py:18
  65.7 2.4 %collective-permute-start.4 = (f32[16,2]{0,1:T(2,128)S(1)}, f32[16,2]{0,1:T(2,128)S(1)}, u32[]{:S(2)}, u32[]{:S(2)}) collective-permute-start(f32[16,2]{0,1:T(2,128)S(1)} %constant_dynamic-slice_fusion.11), channel_id=1, source_target_pairs={{0,8},{8,0},{16,24},{24,16},{32,40},{40,32},{48,56},{56,48},{64,72... | collective-permute-start | bytes 392 | tf_op jit(solution)/shard_map/ppermute | solution.py:18
  65.8 2.4 %collective-permute-start.7 = (f32[16,2]{0,1:T(2,128)S(1)}, f32[16,2]{0,1:T(2,128)S(1)}, u32[]{:S(2)}, u32[]{:S(2)}) collective-permute-start(f32[16,2]{0,1:T(2,128)S(1)} %constant_dynamic-slice_fusion.6), channel_id=1, source_target_pairs={{0,8},{8,0},{16,24},{24,16},{32,40},{40,32},{48,56},{56,48},{64,72... | collective-permute-start | bytes 392 | tf_op jit(solution)/shard_map/ppermute | solution.py:18
  67.3 2.9 %collective-permute-start.5 = (f32[16,128]{1,0:T(8,128)S(1)}, f32[16,128]{1,0:T(8,128)S(1)}, u32[]{:S(2)}, u32[]{:S(2)}) collective-permute-start(f32[16,128]{1,0:T(8,128)S(1)} %constant_dynamic-slice_fusion.10), channel_id=1, source_target_pairs={{0,8},{8,0},{16,24},{24,16},{32,40},{40,32},{48,56},{56,48},{64,72... | collective-permute-start | bytes 24584 | tf_op jit(solution)/shard_map/ppermute | solution.py:18
  71.2 20.3 %all-to-all-start.1 = ((f32[8,16,1024]{2,1,0:T(8,128)}), f32[8,16,1024]{2,1,0:T(8,128)S(1)}, u32[]{:S(2)}, u32[]{:S(2)}) async-start(f32[8,16,1024]{2,1,0:T(8,128)} %broadcast_in_dim.16), calls=%async_computation.1 | async-start | bytes 1048576 | tf_op jit(solution)/shard_map/all_to_all | solution.py:32
  91.5 4.2 %copy-start.1 = (bf16[1,16,32,1024]{3,2,1,0:T(8,128)(2,1)S(1)}, bf16[1,16,32,1024]{3,2,1,0:T(8,128)(2,1)}, u32[]{:S(2)}) copy-start(bf16[1,16,32,1024]{3,2,1,0:T(8,128)(2,1)} %param.28) | copy-start | bytes 3145732
  92.1 2.8 %collective-permute-start.8 = (bf16[16,1024]{1,0:T(8,128)(2,1)S(1)}, bf16[16,1024]{1,0:T(8,128)(2,1)S(1)}, u32[]{:S(2)}, u32[]{:S(2)}) collective-permute-start(bf16[16,1024]{1,0:T(8,128)(2,1)S(1)} %convolution_convert_fusion), channel_id=1, source_target_pairs={{0,8},{8,0},{16,24},{24,16},{32,40},{40,32},{48,56},{56,48},{64,72... | collective-permute-start | bytes 98312 | tf_op jit(solution)/shard_map/ppermute | solution.py:18
  94.8 7.2 %collective-permute-start.9 = (bf16[32,1024]{1,0:T(8,128)(2,1)S(1)}, bf16[32,1024]{1,0:T(8,128)(2,1)S(1)}, u32[]{:S(2)}, u32[]{:S(2)}) collective-permute-start(bf16[32,1024]{1,0:T(8,128)(2,1)S(1)} %maximum_select_fusion.1), channel_id=1, source_target_pairs={{0,16},{8,24},{16,0},{24,8},{32,48},{40,56},{48,32},{56,40},{64,80... | collective-permute-start | bytes 196616 | tf_op jit(solution)/shard_map/ppermute | solution.py:18
  105.5 6.6 %collective-permute-start.10 = (f32[32,16]{0,1:T(8,128)S(1)}, f32[32,16]{0,1:T(8,128)S(1)}, u32[]{:S(2)}, u32[]{:S(2)}) collective-permute-start(f32[32,16]{0,1:T(8,128)S(1)} %constant_dynamic-slice_fusion.5), channel_id=1, source_target_pairs={{0,16},{8,24},{16,0},{24,8},{32,48},{40,56},{48,32},{56,40},{64,80... | collective-permute-start | bytes 6152 | tf_op jit(solution)/shard_map/ppermute | solution.py:18
  108.9 4.0 %collective-permute-start.14 = (f32[32,16]{0,1:T(8,128)S(1)}, f32[32,16]{0,1:T(8,128)S(1)}, u32[]{:S(2)}, u32[]{:S(2)}) collective-permute-start(f32[32,16]{0,1:T(8,128)S(1)} %constant_dynamic-slice_fusion.1), channel_id=1, source_target_pairs={{0,16},{8,24},{16,0},{24,8},{32,48},{40,56},{48,32},{56,40},{64,80... | collective-permute-start | bytes 6152 | tf_op jit(solution)/shard_map/ppermute | solution.py:18
  113.1 3.9 %collective-permute-start.12 = (f32[16,16]{0,1:T(8,128)S(1)}, f32[16,16]{0,1:T(8,128)S(1)}, u32[]{:S(2)}, u32[]{:S(2)}) collective-permute-start(f32[16,16]{0,1:T(8,128)S(1)} %constant_dynamic-slice_fusion.3), channel_id=1, source_target_pairs={{0,8},{8,0},{16,24},{24,16},{32,40},{40,32},{48,56},{56,48},{64,72... | collective-permute-start | bytes 3080 | tf_op jit(solution)/shard_map/ppermute | solution.py:18
  113.8 3.2 %collective-permute-start.15 = (f32[16,16]{0,1:T(8,128)S(1)}, f32[16,16]{0,1:T(8,128)S(1)}, u32[]{:S(2)}, u32[]{:S(2)}) collective-permute-start(f32[16,16]{0,1:T(8,128)S(1)} %constant_dynamic-slice_fusion), channel_id=1, source_target_pairs={{0,8},{8,0},{16,24},{24,16},{32,40},{40,32},{48,56},{56,48},{64,72... | collective-permute-start | bytes 3080 | tf_op jit(solution)/shard_map/ppermute | solution.py:18
  114.7 34.3 %collective-permute-start.11 = (f32[32,1024]{1,0:T(8,128)S(1)}, f32[32,1024]{1,0:T(8,128)S(1)}, u32[]{:S(2)}, u32[]{:S(2)}) collective-permute-start(f32[32,1024]{1,0:T(8,128)S(1)} %constant_dynamic-slice_fusion.4), channel_id=1, source_target_pairs={{0,16},{8,24},{16,0},{24,8},{32,48},{40,56},{48,32},{56,40},{64,80... | collective-permute-start | bytes 393224 | tf_op jit(solution)/shard_map/ppermute | solution.py:18
  149.0 3.3 %collective-permute-start.13 = (f32[16,1024]{1,0:T(8,128)S(1)}, f32[16,1024]{1,0:T(8,128)S(1)}, u32[]{:S(2)}, u32[]{:S(2)}) collective-permute-start(f32[16,1024]{1,0:T(8,128)S(1)} %constant_dynamic-slice_fusion.2), channel_id=1, source_target_pairs={{0,8},{8,0},{16,24},{24,16},{32,40},{40,32},{48,56},{56,48},{64,72... | collective-permute-start | bytes 196616 | tf_op jit(solution)/shard_map/ppermute | solution.py:18
where the time goes:
time: 171 us
  blocking collectives  47.2 us (28%)
  starting transfers between devices  43.5 us (25%)
  waiting for transfers between devices  42.1 us (25%)
  local copies, waits for them, and re-layouts  18 us (11%)
  matrix products  15.6 us (9%)
  other arithmetic  3 us (2%)
    all_gather x6, blocking collectives, combined_by_axis(): pieces = jax.tree.map(lambda part: lax.all_gather(part, axis), x)  47.2 us
    all_to_all x1, waiting for transfers between devices, shards(): lax.all_to_all(owned, 'dp', split_axis=0, concat_axis=0, tiled=True)  26.1 us
    ppermute x16, starting transfers between devices, from_partner(): return lax.ppermute(value, axis, pairs)  20.6 us
    all_to_all x1, starting transfers between devices, shards(): lax.all_to_all(owned, 'dp', split_axis=0, concat_axis=0, tiled=True)  12 us
    all_to_all x1, starting transfers between devices, copy_for_each(): return lax.all_to_all(copies, axis, split_axis=0, concat_axis=0, tiled=True)  10.9 us
    all_to_all x1, waiting for transfers between devices, copy_for_each(): return lax.all_to_all(copies, axis, split_axis=0, concat_axis=0, tiled=True)  9.34 us
    ppermute x16, waiting for transfers between devices, from_partner(): return lax.ppermute(value, axis, pairs)  6.63 us
    dot_general x1, matrix products, shards(): jnp.dot(onehot_table, embedding, preferred_element_type=jnp.float32)  4.02 us
  transfers between devices with their start and end apart: 18, of which 9 were waited for; matrix products, arithmetic and copies ran while one was open for 12% of the time, Pallas kernels for 0%

commit v1 on v0

v1 whole, which is shorter than its diff:
```python
import jax
import jax.numpy as jnp
from jax import lax
from jax.experimental import pallas as pl
from jax.experimental.pallas import tpu as pltpu
from jax.sharding import PartitionSpec as P

MESH = pl.DeviceIdType.MESH
F32 = jnp.float32
BF16 = jnp.bfloat16

D = 1024
CHUNKS = 8
BEAMS = 4
IMAGES = 16
ROWS = BEAMS * IMAGES
DP = 32
PATCH = 8
PLANE = 32
SLAB = 1000
LEN = 128
SPOTS = 32
NEG = -1e30
NT = (((1,), (1,)), ((), ()))


def dot(a, b):
    return jnp.dot(a, b, preferred_element_type=F32)


def dot_nt(a, b):
    return lax.dot_general(a, b, NT, preferred_element_type=F32)


def tree(parts):
    while len(parts) > 1:
        parts = [a + b for a, b in zip(parts[::2], parts[1::2])] + (
            [parts[-1]] if len(parts) % 2 else []
        )
    return parts[0]


def loop(count, step):
    def body(k, carry):
        step(k)
        return carry

    lax.fori_loop(1, count, body, 0)


def split_heads(x):
    lane = lax.broadcasted_iota(jnp.int32, x.shape, 1)
    low = jnp.where(lane < 64, x, 0.0)
    high = jnp.where(lane < 64, 0.0, x)
    return jnp.concatenate([low, high], axis=0).astype(BF16)


def join_heads(x):
    half = x.shape[0] // 2
    lane = lax.broadcasted_iota(jnp.int32, (half, 128), 1)
    return jnp.where(lane < 64, x[:half], x[half:])


def kernel(
    ids_ref,
    parents_ref,
    emb_ref,
    sgain_ref,
    wq_ref,
    wk_ref,
    wv_ref,
    wo_ref,
    pk_ref,
    pv_ref,
    cgain_ref,
    cq_ref,
    co_ref,
    ik_ref,
    iv_ref,
    hidden_ref,
    newk_ref,
    newv_ref,
    emb,
    wqkv,
    wo,
    pk,
    pv,
    cq,
    co,
    ik,
    iv,
    owned,
    r1,
    tokc,
    r2,
    tokf,
    masks,
    part,
    r4,
    row_f,
    prob,
    r5,
    probf,
    num,
    r6,
    stat,
    r6s,
    hid,
    r7,
    hidf,
    load_sem,
    send_sem,
    recv_sem,
):
    d = lax.axis_index("dp")
    p = lax.axis_index("patch")
    z = d // 4
    x = d % 4
    q = x * 8 + p

    barrier = pltpu.get_barrier_semaphore()

    def greet_dp(k):
        pl.semaphore_signal(barrier, inc=1, device_id=((d + k) % DP, p), device_id_type=MESH)

    def plane_id(k):
        to = (q + k) % PLANE
        return to, (z * 4 + to // 8, to % 8)

    def greet_plane(k):
        to, device = plane_id(k)
        pl.semaphore_signal(barrier, inc=1, device_id=device, device_id_type=MESH)

    loop(DP, greet_dp)
    loop(PLANE, greet_plane)

    emb[992:1024, :] = jnp.zeros((32, 128), BF16)

    loads = []

    def load(src, dst):
        copy = pltpu.make_async_copy(src, dst, load_sem.at[len(loads)])
        copy.start()
        loads.append(copy)
        return copy

    l_emb = load(emb_ref.at[:, pl.ds(pl.multiple_of(p * 128, 128), 128)], emb.at[pl.ds(0, SLAB), :])
    l_q = load(wq_ref, wqkv.at[:, 0:128])
    l_k = load(wk_ref, wqkv.at[:, 128:256])
    l_v = load(wv_ref, wqkv.at[:, 256:384])
    l_pk = load(pk_ref, pk)
    l_pv = load(pv_ref, pv)
    l_wo = load(wo_ref, wo)
    l_cq = load(cq_ref, cq)
    l_ik = load(ik_ref, ik)
    l_iv = load(iv_ref, iv)
    l_co = load(co_ref, co)

    r256 = lax.broadcasted_iota(jnp.int32, (256, 128), 0)
    masks[...] = jnp.where(r256 // 16 == r256 % 16, 1.0, 0.0).astype(BF16)
    row_f[...] = jnp.zeros((64, 128), F32)

    l_emb.wait()
    lane1024 = lax.broadcasted_iota(jnp.int32, (128, 1024), 1)
    for c in range(4):
        col = jnp.broadcast_to(ids_ref[c : c + 1, :], (128, 128)).T - d * SLAB
        wide = jnp.concatenate([col] * 8, axis=1)
        onehot = jnp.where(wide == lane1024, 1.0, 0.0).astype(BF16)
        owned[c * 128 : (c + 1) * 128, :] = dot(onehot, emb[...]).astype(BF16)

    pl.semaphore_wait(barrier, (DP - 1) + (PLANE - 1))

    def await_bytes(ref, sem):
        pltpu.make_async_copy(ref, ref, sem).wait()

    def send1(k):
        to = (d + k) % DP
        pltpu.make_async_remote_copy(
            src_ref=owned.at[pl.ds(pl.multiple_of(to * 16, 16), 16), :],
            dst_ref=r1.at[d],
            send_sem=send_sem.at[0],
            recv_sem=recv_sem.at[0],
            device_id=(to, p),
            device_id_type=MESH,
        ).start()

    loop(DP, send1)
    r1[d] = owned[pl.ds(pl.multiple_of(d * 16, 16), 16), :]
    await_bytes(r1.at[pl.ds(0, DP - 1)], recv_sem.at[0])
    chunk = tree([r1[s] for s in range(DP)])
    tokc[...] = chunk
    r2[q] = chunk

    def send_plane(src_of, dst, n):
        def send(k):
            to, device = plane_id(k)
            pltpu.make_async_remote_copy(
                src_ref=src_of(to),
                dst_ref=dst.at[q],
                send_sem=send_sem.at[n],
                recv_sem=recv_sem.at[n],
                device_id=device,
                device_id_type=MESH,
            ).start()

        loop(PLANE, send)

    def await_plane(dst, n):
        await_bytes(dst.at[pl.ds(0, PLANE - 1)], recv_sem.at[n])

    send_plane(lambda to: tokc, r2, 1)
    l_q.wait()
    l_k.wait()
    l_v.wait()
    await_plane(r2, 1)

    toks = [
        jnp.concatenate([r2[b * 8 + j] for b in range(BEAMS)], axis=0).astype(F32)
        for j in range(CHUNKS)
    ]
    for j in range(CHUNKS):
        tokf[pl.ds(j, ROWS, stride=8), :] = toks[j]
    square = tree([t * t for t in toks])
    factor = lax.rsqrt(jnp.sum(square, axis=1, keepdims=True) * (1.0 / D) + 1e-06)
    sgain = sgain_ref[...].astype(F32)
    normed = jnp.concatenate(
        [(toks[j] * factor * sgain[j : j + 1, :]).astype(BF16) for j in range(CHUNKS)], axis=1
    )
    qkv = dot(normed, wqkv[...]).astype(BF16)
    tokf_q, tokf_k, tokf_v = (qkv[:, n * 128 : (n + 1) * 128].astype(F32) for n in range(3))
    queries = split_heads(tokf_q)
    own = jnp.sum(
        queries.astype(F32) * jnp.concatenate([tokf_k, tokf_k], axis=0), axis=1, keepdims=True
    )
    own = own * 0.125
    beam_row = pl.ds(pl.multiple_of(x * 16, 16), 16)
    num[0:ROWS, :] = tokf_k
    num[ROWS : 2 * ROWS, :] = tokf_v
    newk_ref[...] = num[beam_row, :].astype(BF16)
    newv_ref[...] = num[pl.ds(pl.multiple_of(ROWS + x * 16, 16), 16), :].astype(BF16)

    mask_of = [masks[i * 16 : (i + 1) * 16, :] for i in range(IMAGES)]

    def only(value, i):
        return (value.reshape(8, 16, 128) * mask_of[i][None]).reshape(128, 128)

    l_pk.wait()
    scores = tree(
        [dot_nt(only(queries, i), pk[i * LEN : (i + 1) * LEN, :]) for i in range(IMAGES)]
    )
    scores = scores * 0.125
    peak = jnp.maximum(jnp.max(scores, axis=1, keepdims=True), own)
    powers = jnp.exp(scores - peak)
    own_power = jnp.exp(own - peak)
    total = jnp.sum(powers, axis=1, keepdims=True) + own_power
    weights = powers.astype(BF16)
    own_weight = own_power.astype(BF16).astype(F32)
    l_pv.wait()
    context = tree(
        [dot(only(weights, i), pv[i * LEN : (i + 1) * LEN, :]) for i in range(IMAGES)]
    )
    context = (context + own_weight * jnp.concatenate([tokf_v, tokf_v], axis=0)) / total
    context = join_heads(context)
    pcol = jnp.broadcast_to(parents_ref[pl.ds(z // 2, 1), :], (128, 128)).T
    pcol = jnp.where(z % 2 == 0, pcol[:ROWS], pcol[ROWS:])
    context = jnp.where(pcol == x, context, 0.0).astype(BF16)

    l_wo.wait()
    projected = dot(context, wo[...])
    for j in range(CHUNKS):
        part[pl.ds(j, ROWS, stride=8), :] = projected[:, j * 128 : (j + 1) * 128]
    mine = pl.ds(pl.multiple_of(q * 16, 16), 16)

    def part_of(to):
        return part.at[pl.ds(pl.multiple_of(to * 16, 16), 16), :]

    send_plane(part_of, r4, 2)
    r4[q] = part[mine, :]
    l_cq.wait()
    await_plane(r4, 2)
    middle = tree([r4[s] for s in range(PLANE)]) + tokf[mine, :]

    cgain = cgain_ref[...].astype(F32)
    for r in range(2):
        row = middle[r * 8 : (r + 1) * 8, :]
        factor = lax.rsqrt(jnp.sum(row * row, keepdims=True) * (1.0 / D) + 1e-06)
        row_f[r * 8 : (r + 1) * 8, :] = row * factor * cgain

    def two_rows():
        return jnp.concatenate(
            [row_f[pl.ds(j, 8, stride=8), :] for j in range(CHUNKS)], axis=1
        ).astype(BF16)

    def back(value):
        for j in range(CHUNKS):
            row_f[pl.ds(j, 8, stride=8), :] = value[:, j * 128 : (j + 1) * 128]
        return row_f[0:16, :]

    mine_probe = back(dot(two_rows(), cq[...])).astype(BF16)
    prob[...] = mine_probe
    r5[q] = mine_probe

    send_plane(lambda to: prob, r5, 3)
    l_ik.wait()
    l_iv.wait()
    await_plane(r5, 3)
    probf[...] = r5[...].astype(F32).reshape(512, 128)

    same = lax.broadcasted_iota(jnp.int32, (128, 512), 0) % IMAGES == (
        lax.broadcasted_iota(jnp.int32, (128, 512), 1) // SPOTS
    )
    lane = lax.broadcasted_iota(jnp.int32, (ROWS, 128), 1)
    stats = jnp.zeros((ROWS, 128), F32)
    for j in range(CHUNKS):
        probes = split_heads(probf[pl.ds(j, ROWS, stride=8), :])
        block = slice(j * 128, (j + 1) * 128)
        scores = dot_nt(probes, ik[:, block]) * 0.125
        scores = jnp.where(same, scores, NEG)
        peak = jnp.max(scores, axis=1, keepdims=True)
        powers = jnp.exp(scores - peak)
        total = jnp.sum(powers, axis=1, keepdims=True)
        summed = join_heads(dot(powers.astype(BF16), iv[:, block]))
        num[pl.ds(j, ROWS, stride=8), :] = summed
        for h in range(2):
            rows = slice(h * ROWS, (h + 1) * ROWS)
            stats = jnp.where(lane == h * 8 + j, peak[rows], stats)
            stats = jnp.where(lane == 16 + h * 8 + j, total[rows], stats)
    stat[...] = stats

    def num_of(to):
        return num.at[pl.ds(pl.multiple_of(to * 16, 16), 16), :]

    def stat_of(to):
        return stat.at[pl.ds(pl.multiple_of(to * 2, 2), 2), :]

    send_plane(stat_of, r6s, 5)
    send_plane(num_of, r6, 4)
    r6[q] = num[mine, :]
    r6s[q] = stat[pl.ds(pl.multiple_of(q * 2, 2), 2), :]
    l_co.wait()
    await_plane(r6s, 5)
    stats = jnp.concatenate(
        [r6s[...].reshape(64, 128), jnp.zeros((64, 128), F32)], axis=0
    ).T
    lane8 = lax.broadcasted_iota(jnp.int32, (8, 128), 1)
    shares = []
    for r in range(2):
        valid = (lane8 < 64) & (lane8 % 2 == r)
        pair = []
        for h in range(2):
            peaks = jnp.where(valid, stats[h * 8 : (h + 1) * 8, :], NEG)
            totals = stats[16 + h * 8 : 16 + (h + 1) * 8, :]
            scale = jnp.where(valid, jnp.exp(peaks - jnp.max(peaks, axis=1, keepdims=True)), 0.0)
            pair.append((scale, jnp.sum(scale * totals, axis=1, keepdims=True)))
        shares.append(pair)
    await_plane(r6, 4)
    low = lane8 < 64
    for r in range(2):
        (scale0, total0), (scale1, total1) = shares[r]
        terms = []
        for s in range(PLANE):
            at = slice(2 * s + r, 2 * s + r + 1)
            scale = jnp.where(low, scale0[:, at], scale1[:, at])
            terms.append(r6[s, r * 8 : (r + 1) * 8, :] * scale)
        row_f[r * 8 : (r + 1) * 8, :] = tree(terms) / jnp.where(low, total0, total1)
    final = (back(dot(two_rows(), co[...])) + middle).astype(BF16)
    hid[...] = final
    r7[p] = final

    def send7(k):
        to = (p + k) % PATCH
        pltpu.make_async_remote_copy(
            src_ref=hid,
            dst_ref=r7.at[p],
            send_sem=send_sem.at[6],
            recv_sem=recv_sem.at[6],
            device_id=(d, to),
            device_id_type=MESH,
        ).start()

    loop(PATCH, send7)
    await_bytes(r7.at[pl.ds(0, PATCH - 1)], recv_sem.at[6])
    hidf[...] = r7[...].astype(F32).reshape(128, 128)
    for j in range(CHUNKS):
        hidden_ref[:, j * 128 : (j + 1) * 128] = hidf[pl.ds(j, 16, stride=8), :].astype(BF16)

    for n, ref in enumerate((r1, r2, r4, r5, r6, r6s)):
        await_bytes(ref.at[pl.ds(0, 31)], send_sem.at[n])
    await_bytes(r7.at[pl.ds(0, PATCH - 1)], send_sem.at[6])


def shards(
    token_ids,
    parents,
    embedding,
    self_gain,
    query_weight,
    key_weight,
    value_weight,
    output_weight,
    past_keys,
    past_values,
    cross_gain,
    cross_query,
    cross_output,
    image_keys,
    image_values,
):
    vmem = pl.BlockSpec(memory_space=pltpu.VMEM)
    hbm = pl.BlockSpec(memory_space=pl.ANY)
    return pl.pallas_call(
        kernel,
        out_shape=(
            jax.ShapeDtypeStruct((16, D), BF16),
            jax.ShapeDtypeStruct((16, 128), BF16),
            jax.ShapeDtypeStruct((16, 128), BF16),
        ),
        in_specs=[vmem, vmem, hbm, vmem, hbm, hbm, hbm, hbm, hbm, hbm, vmem, hbm, hbm, hbm, hbm],
        out_specs=(vmem, vmem, vmem),
        scratch_shapes=[
            pltpu.VMEM((1024, 128), BF16),
            pltpu.VMEM((D, 384), BF16),
            pltpu.VMEM((128, D), BF16),
            pltpu.VMEM((2048, 128), BF16),
            pltpu.VMEM((2048, 128), BF16),
            pltpu.VMEM((D, D), BF16),
            pltpu.VMEM((D, D), BF16),
            pltpu.VMEM((512, D), BF16),
            pltpu.VMEM((512, D), BF16),
            pltpu.VMEM((512, 128), BF16),
            pltpu.VMEM((DP, 16, 128), BF16),
            pltpu.VMEM((16, 128), BF16),
            pltpu.VMEM((PLANE, 16, 128), BF16),
            pltpu.VMEM((512, 128), F32),
            pltpu.VMEM((256, 128), BF16),
            pltpu.VMEM((512, 128), F32),
            pltpu.VMEM((PLANE, 16, 128), F32),
            pltpu.VMEM((64, 128), F32),
            pltpu.VMEM((16, 128), BF16),
            pltpu.VMEM((PLANE, 16, 128), BF16),
            pltpu.VMEM((512, 128), F32),
            pltpu.VMEM((512, 128), F32),
            pltpu.VMEM((PLANE, 16, 128), F32),
            pltpu.VMEM((ROWS, 128), F32),
            pltpu.VMEM((PLANE, 2, 128), F32),
            pltpu.VMEM((16, 128), BF16),
            pltpu.VMEM((PATCH, 16, 128), BF16),
            pltpu.VMEM((128, 128), F32),
            pltpu.SemaphoreType.DMA((11,)),
            pltpu.SemaphoreType.DMA((7,)),
            pltpu.SemaphoreType.DMA((7,)),
        ],
        compiler_params=pltpu.CompilerParams(collective_id=0, has_side_effects=True),
        name="step",
    )(
        token_ids.reshape(4, 128),
        parents.reshape(4, 128),
        embedding,
        self_gain.reshape(8, 128),
        query_weight,
        key_weight,
        value_weight,
        output_weight,
        past_keys.reshape(2048, 128),
        past_values.reshape(2048, 128),
        cross_gain.reshape(8, 128),
        cross_query,
        cross_output,
        image_keys.reshape(512, D),
        image_values.reshape(512, D),
    )


def solution(mesh):
    in_specs = (
        P(),
        P(),
        P("dp", None),
        P(),
        P(None, "patch"),
        P(None, "patch"),
        P(None, "patch"),
        P("patch", None),
        P("dp", None, "patch"),
        P("dp", None, "patch"),
        P(),
        P(),
        P(),
        P("dp", None, "patch", None),
        P("dp", None, "patch", None),
    )
    out_specs = (P("dp", None), P("dp", "patch"), P("dp", "patch"))
    return jax.shard_map(
        shards, mesh=mesh, in_specs=in_specs, out_specs=out_specs, check_vma=False
    )
```

time: 171 us -> 58.1 us (0.34)
  Pallas kernels: 0 us -> 53.3 us
  blocking collectives: 47.2 us -> 0 us
  starting transfers between devices: 43.5 us -> 0 us
  waiting for transfers between devices: 42.1 us -> 0 us
  matrix products: 15.6 us -> 0 us
  local copies, waits for them, and re-layouts: 18 us -> 3.91 us
  other arithmetic: 3 us -> 0 us
    pallas_call x0 -> x1, Pallas kernels: none -> 53.3 us  [shards(): pl.pallas_call(kernel, out_shape=(jax.ShapeDtypeStruct((16, D), BF16), ja...]
    all_gather x6 -> x0, blocking collectives: 47.2 us -> none  [combined_by_axis(): pieces = jax.tree.map(lambda part: lax.all_gather(part, axis), x)]
    all_to_all x2 -> x0, waiting for transfers between devices: 35.5 us -> none  [the longest x1 26.1 us: shards(): lax.all_to_all(owned, 'dp', split_axis=0, concat_axis=0, tiled=True)]
    all_to_all x2 -> x0, starting transfers between devices: 22.9 us -> none  [the longest x1 12 us: shards(): lax.all_to_all(owned, 'dp', split_axis=0, concat_axis=0, tiled=True)]
    ppermute x16 -> x0, starting transfers between devices: 20.6 us -> none  [from_partner(): return lax.ppermute(value, axis, pairs)]
    dot_general x11 -> x0, matrix products: 15.6 us -> none  [the longest x1 4.02 us: shards(): jnp.dot(onehot_table, embedding, preferred_element_type=jnp.float32)]
    reshape x6 -> x0, local copies, waits for them, and re-layouts: 6.77 us -> none  [the longest x1 4.01 us: shards(): image_values.reshape(row_count, patch_count, HEADS, head_size)]
    ppermute x16 -> x0, waiting for transfers between devices: 6.63 us -> none  [from_partner(): return lax.ppermute(value, axis, pairs)]
  transfers between devices with their start and end apart: 18 -> 0, of which waited for: 9 -> 0; matrix products, arithmetic and copies ran while one was open for 12% -> 0% of each run, Pallas kernels for 0% -> 0%
where the time goes in v1:
time: 58.1 us; the launch traced here: 57.9 us
  Pallas kernels  53.3 us (92%)
  local copies, waits for them, and re-layouts  3.91 us (7%)
  between operations  0.65 us (1%)
    pallas_call x1, Pallas kernels, shards(): pl.pallas_call(kernel, out_shape=(jax.ShapeDtypeStruct((16, D), BF16), ja...  53.3 us
    unnamed x3, local copies, waits for them, and re-layouts  3.91 us

profile of v1, /device:TPU:1, one launch (start us, length us, event | category | flops | bytes accessed | tf_op | source)
XLA Modules:
  0.0 57.9 jit_solution(17298062118898562579)
XLA Ops:
  0.6 53.3 %step.1 = (bf16[16,1024]{1,0:T(8,128)(2,1)}, bf16[16,128]{1,0:T(8,128)(2,1)}, bf16[16,128]{1,0:T(8,128)(2,1)}) custom-call(s32[4,128]{1,0:T(4,128)} %bitcast.12, s32[4,128]{1,0:T(4,128)} %bitcast.13, bf16[1000,1024]{1,0:T(8,128)(2,1)} %emb_ref.1, bf16[8,128]{1,0:T(8,128)(2,1)} %bitcast.14, bf16[1024,128]{1,0:T(8,128)(2,1)} %wq_ref.1, ...), custom_call_target="tpu_custom_call" | custom-call | tf_op jit(solution)/shard_map/step/pallas_call | solution.py:411
  54.0 1.4 %copy.21 = bf16[16,1024]{1,0:T(8,128)(2,1)} copy(bf16[16,1024]{1,0:T(8,128)(2,1)} %get-tuple-element.6) | data formatting | bytes 65536
  55.3 1.3 %copy.22 = bf16[16,128]{1,0:T(8,128)(2,1)} copy(bf16[16,128]{1,0:T(8,128)(2,1)} %get-tuple-element.7) | data formatting | bytes 8192
  56.6 1.3 %copy.23 = bf16[16,128]{1,0:T(8,128)(2,1)} copy(bf16[16,128]{1,0:T(8,128)(2,1)} %get-tuple-element.8) | data formatting | bytes 8192

commit v2 on v1

v2 whole, which is shorter than its diff:
```python
import jax
import jax.numpy as jnp
from jax import lax
from jax.experimental import pallas as pl
from jax.experimental.pallas import tpu as pltpu
from jax.sharding import PartitionSpec as P

MESH = pl.DeviceIdType.MESH
F32 = jnp.float32
BF16 = jnp.bfloat16

D = 1024
CHUNKS = 8
BEAMS = 4
IMAGES = 16
ROWS = BEAMS * IMAGES
DP = 32
PATCH = 8
PLANE = 32
SLAB = 1000
LEN = 128
SPOTS = 32
NEG = -1e30
NT = (((1,), (1,)), ((), ()))


def dot(a, b):
    return jnp.dot(a, b, preferred_element_type=F32)


def dot_nt(a, b):
    return lax.dot_general(a, b, NT, preferred_element_type=F32)


def tree(parts):
    while len(parts) > 1:
        parts = [a + b for a, b in zip(parts[::2], parts[1::2])] + (
            [parts[-1]] if len(parts) % 2 else []
        )
    return parts[0]


def hops(step, size):
    return min(step, size - step)


PARTNERS = sorted(
    [(dx, dy, dc) for dx in range(4) for dy in range(4) for dc in range(2) if dx + dy + dc],
    key=lambda t: -hops(t[0], 4) - hops(t[1], 4),
)
ACROSS = (2, 1, 3, 0)


def split_heads(x):
    lane = lax.broadcasted_iota(jnp.int32, x.shape, 1)
    low = jnp.where(lane < 64, x, 0.0)
    high = jnp.where(lane < 64, 0.0, x)
    return jnp.concatenate([low, high], axis=0).astype(BF16)


def join_heads(x):
    half = x.shape[0] // 2
    lane = lax.broadcasted_iota(jnp.int32, (half, 128), 1)
    return jnp.where(lane < 64, x[:half], x[half:])


def kernel(
    ids_hbm,
    parents_hbm,
    emb_ref,
    sgain_hbm,
    wq_ref,
    wk_ref,
    wv_ref,
    wo_ref,
    pk_ref,
    pv_ref,
    cgain_hbm,
    cq_ref,
    co_ref,
    ik_ref,
    iv_ref,
    hidden_ref,
    newk_ref,
    newv_ref,
    ids_ref,
    parents_ref,
    sgain_ref,
    cgain_ref,
    emb,
    wqkv,
    wo,
    pk,
    pv,
    cq,
    co,
    ik,
    iv,
    onehot,
    owned,
    r1,
    tokc,
    r2,
    tokf,
    masks,
    part,
    partb,
    r4,
    row_f,
    prob,
    r5,
    probf,
    num,
    numb,
    r6,
    stat,
    r6s,
    hid,
    r7,
    hidf,
    load_sem,
    send_sem,
    recv_sem,
    ready,
):
    d = lax.axis_index("dp")
    p = lax.axis_index("patch")
    z, x = d // 4, d % 4
    y, c = p // 2, p % 2
    q = x * 8 + p
    zs = [lax.rem(z + k, 8) for k in range(8)]
    xs = [lax.rem(x + k, 4) for k in range(4)]
    ys = [lax.rem(y + k, 4) for k in range(4)]
    cs = [c, 1 - c]

    loads = []

    def load(src, dst):
        copy = pltpu.make_async_copy(src, dst, load_sem.at[len(loads)])
        copy.start()
        loads.append(copy)
        return copy

    emb[992:1024, :] = jnp.zeros((32, 128), BF16)
    l_ids = load(ids_hbm, ids_ref)
    l_emb = load(emb_ref.at[:, pl.ds(pl.multiple_of(p * 128, 128), 128)], emb.at[pl.ds(0, SLAB), :])

    barrier = pltpu.get_barrier_semaphore()

    def signal(sem, device):
        pl.semaphore_signal(sem, inc=1, device_id=device, device_id_type=MESH)

    for dz in range(1, 8):

        @pl.when(z + dz < 8)
        def _(dz=dz):
            for dx in ACROSS:
                signal(barrier, (zs[dz] * 4 + xs[dx], p))

    for dx, dy, dc in PARTNERS:
        signal(barrier, (z * 4 + xs[dx], ys[dy] * 2 + cs[dc]))

    l_q = load(wq_ref, wqkv.at[:, 0:128])
    l_k = load(wk_ref, wqkv.at[:, 128:256])
    l_v = load(wv_ref, wqkv.at[:, 256:384])
    l_gain = load(sgain_hbm, sgain_ref)
    l_parents = load(parents_hbm, parents_ref)
    l_pk = load(pk_ref, pk)
    l_pv = load(pv_ref, pv)
    l_wo = load(wo_ref, wo)
    l_cgain = load(cgain_hbm, cgain_ref)
    l_cq = load(cq_ref, cq)
    l_ik = load(ik_ref, ik)
    l_iv = load(iv_ref, iv)
    l_co = load(co_ref, co)

    r256 = lax.broadcasted_iota(jnp.int32, (256, 128), 0)
    masks[...] = jnp.where(r256 // 16 == r256 % 16, 1.0, 0.0).astype(BF16)
    row_f[...] = jnp.zeros((64, 128), F32)

    l_ids.wait()
    lane1024 = lax.broadcasted_iota(jnp.int32, (128, 1024), 1)
    for n in range(4):
        col = jnp.broadcast_to(ids_ref[n : n + 1, :], (128, 128)).T - d * SLAB
        wide = jnp.concatenate([col] * 8, axis=1)
        onehot[n * 128 : (n + 1) * 128, :] = jnp.where(wide == lane1024, 1.0, 0.0).astype(BF16)
    l_emb.wait()
    for n in range(4):
        rows = slice(n * 128, (n + 1) * 128)
        owned[rows, :] = dot(onehot[rows, :], emb[...]).astype(BF16)

    pl.semaphore_wait(barrier, (PLANE - 1) + 4 * z)
    for dz in range(1, 8):

        @pl.when(z + dz >= 8)
        def _(dz=dz):
            for dx in ACROSS:
                signal(ready.at[z], (zs[dz] * 4 + xs[dx], p))

    def await_bytes(ref, sem):
        pltpu.make_async_copy(ref, ref, sem).wait()

    def send1(dz, dx):
        to = zs[dz] * 4 + xs[dx]
        pltpu.make_async_remote_copy(
            src_ref=owned.at[pl.ds(pl.multiple_of(to * 16, 16), 16), :],
            dst_ref=r1.at[d],
            send_sem=send_sem.at[0],
            recv_sem=recv_sem.at[0],
            device_id=(to, p),
            device_id_type=MESH,
        ).start()

    for dz in (4, 3, 5, 2, 6, 1, 7):

        @pl.when(z + dz >= 8)
        def _(dz=dz):
            for dx in ACROSS:
                send1(dz, dx)

    for dx in ACROSS[:3]:
        send1(0, dx)
    for dz in range(1, 8):

        @pl.when(z + dz < 8)
        def _(dz=dz):
            pl.semaphore_wait(ready.at[zs[dz]], 4)
            for dx in ACROSS:
                send1(dz, dx)

    r1[d] = owned[pl.ds(pl.multiple_of(d * 16, 16), 16), :]
    await_bytes(r1.at[pl.ds(0, DP - 1)], recv_sem.at[0])
    chunk = tree([r1[s] for s in range(DP)])
    tokc[...] = chunk
    r2[q] = chunk

    def send_plane(src_of, dst, n, partners=PARTNERS):
        for dx, dy, dc in partners:
            to_x, to_p = xs[dx], ys[dy] * 2 + cs[dc]
            pltpu.make_async_remote_copy(
                src_ref=src_of(to_x, to_p),
                dst_ref=dst,
                send_sem=send_sem.at[n],
                recv_sem=recv_sem.at[n],
                device_id=(z * 4 + to_x, to_p),
                device_id_type=MESH,
            ).start()

    def await_plane(dst, n):
        await_bytes(dst.at[pl.ds(0, PLANE - 1)], recv_sem.at[n])

    send_plane(lambda to_x, to_p: tokc, r2.at[q], 1)
    l_q.wait()
    l_k.wait()
    l_v.wait()
    l_gain.wait()
    await_plane(r2, 1)

    toks = [
        jnp.concatenate([r2[b * 8 + j] for b in range(BEAMS)], axis=0).astype(F32)
        for j in range(CHUNKS)
    ]
    for j in range(CHUNKS):
        tokf[pl.ds(j, ROWS, stride=8), :] = toks[j]
    square = tree([t * t for t in toks])
    factor = lax.rsqrt(jnp.sum(square, axis=1, keepdims=True) * (1.0 / D) + 1e-06)
    sgain = sgain_ref[...].astype(F32)
    normed = jnp.concatenate(
        [(toks[j] * factor * sgain[j : j + 1, :]).astype(BF16) for j in range(CHUNKS)], axis=1
    )
    qkv = dot(normed, wqkv[...]).astype(BF16)
    new_q, new_k, new_v = (qkv[:, n * 128 : (n + 1) * 128].astype(F32) for n in range(3))
    queries = split_heads(new_q)
    own = jnp.sum(
        queries.astype(F32) * jnp.concatenate([new_k, new_k], axis=0), axis=1, keepdims=True
    )
    own = own * 0.125
    hidf[0:ROWS, :] = new_k
    hidf[ROWS : 2 * ROWS, :] = new_v
    newk_ref[...] = hidf[pl.ds(pl.multiple_of(x * 16, 16), 16), :].astype(BF16)
    newv_ref[...] = hidf[pl.ds(pl.multiple_of(ROWS + x * 16, 16), 16), :].astype(BF16)

    mask_of = [masks[i * 16 : (i + 1) * 16, :] for i in range(IMAGES)]

    def only(value, i):
        return (value.reshape(8, 16, 128) * mask_of[i][None]).reshape(128, 128)

    l_pk.wait()
    scores = tree(
        [dot_nt(only(queries, i), pk[i * LEN : (i + 1) * LEN, :]) for i in range(IMAGES)]
    )
    scores = scores * 0.125
    peak = jnp.maximum(jnp.max(scores, axis=1, keepdims=True), own)
    powers = jnp.exp(scores - peak)
    own_power = jnp.exp(own - peak)
    total = jnp.sum(powers, axis=1, keepdims=True) + own_power
    weights = powers.astype(BF16)
    own_weight = own_power.astype(BF16).astype(F32)
    l_pv.wait()
    context = tree(
        [dot(only(weights, i), pv[i * LEN : (i + 1) * LEN, :]) for i in range(IMAGES)]
    )
    context = (context + own_weight * jnp.concatenate([new_v, new_v], axis=0)) / total
    context = join_heads(context)
    l_parents.wait()
    pcol = jnp.broadcast_to(parents_ref[pl.ds(z // 2, 1), :], (128, 128)).T
    pcol = jnp.where(z % 2 == 0, pcol[:ROWS], pcol[ROWS:])
    context = jnp.where(pcol == x, context, 0.0).astype(BF16)

    l_wo.wait()
    projected = dot(context, wo[...])
    for j in range(CHUNKS):
        part[pl.ds(j, ROWS, stride=8), :] = projected[:, j * 128 : (j + 1) * 128]
    partb[...] = part[...].astype(BF16)
    mine = pl.ds(pl.multiple_of(q * 16, 16), 16)

    def part_of(to_x, to_p):
        return partb.at[pl.ds(pl.multiple_of((to_x * 8 + to_p) * 16, 16), 16), :]

    send_plane(part_of, r4.at[q], 2)
    r4[q] = partb[mine, :]
    l_cgain.wait()
    l_cq.wait()
    await_plane(r4, 2)
    middle = tree([r4[s].astype(F32) for s in range(PLANE)]) + tokf[mine, :]

    cgain = cgain_ref[...].astype(F32)
    for r in range(2):
        row = middle[r * 8 : (r + 1) * 8, :]
        factor = lax.rsqrt(jnp.sum(row * row, keepdims=True) * (1.0 / D) + 1e-06)
        row_f[r * 8 : (r + 1) * 8, :] = row * factor * cgain

    def two_rows():
        return jnp.concatenate(
            [row_f[pl.ds(j, 8, stride=8), :] for j in range(CHUNKS)], axis=1
        ).astype(BF16)

    def back(value):
        for j in range(CHUNKS):
            row_f[pl.ds(j, 8, stride=8), :] = value[:, j * 128 : (j + 1) * 128]
        return row_f[0:16, :]

    mine_probe = back(dot(two_rows(), cq[...])).astype(BF16)
    prob[...] = mine_probe
    slot = p * 4 + x
    r5[slot] = mine_probe

    send_plane(lambda to_x, to_p: prob, r5.at[slot], 3)
    l_ik.wait()
    l_iv.wait()
    await_plane(r5, 3)

    row32 = lax.broadcasted_iota(jnp.int32, (32, 128), 0)
    image = (row32 // 8 % 2) * 2 + row32 % 2
    same = image == lax.broadcasted_iota(jnp.int32, (32, 128), 1) // SPOTS
    lane = lax.broadcasted_iota(jnp.int32, (16, 128), 1)
    for g, dy in enumerate(ACROSS):
        base = pl.multiple_of(ys[dy] * 128, 128)
        here = slice(g * 128, (g + 1) * 128)
        probf[here, :] = r5[pl.ds(ys[dy] * 8, 8)].astype(F32).reshape(128, 128)
        stats = jnp.zeros((16, 128), F32)
        for j in range(CHUNKS):
            block = slice(j * 128, (j + 1) * 128)
            probes = split_heads(probf[pl.ds(g * 128 + j, 16, stride=8), :])
            scores = dot_nt(probes, ik[pl.ds(base, 128), block]) * 0.125
            scores = jnp.where(same, scores, NEG)
            peak = jnp.max(scores, axis=1, keepdims=True)
            powers = jnp.exp(scores - peak)
            total = jnp.sum(powers, axis=1, keepdims=True)
            summed = join_heads(dot(powers.astype(BF16), iv[pl.ds(base, 128), block]))
            num[pl.ds(g * 128 + j, 16, stride=8), :] = summed
            for h in range(2):
                rows = slice(h * 16, (h + 1) * 16)
                stats = jnp.where(lane == h * 8 + j, peak[rows], stats)
                stats = jnp.where(lane == 16 + h * 8 + j, total[rows], stats)
        stat[g * 16 : (g + 1) * 16, :] = stats
        numb[here, :] = num[here, :].astype(BF16)

        def num_of(to_x, to_p, g=g):
            at = g * 128 + ((to_p % 2) * 4 + to_x) * 16
            return numb.at[pl.ds(pl.multiple_of(at, 16), 16), :]

        def stat_of(to_x, to_p, g=g):
            at = g * 16 + ((to_p % 2) * 4 + to_x) * 2
            return stat.at[pl.ds(pl.multiple_of(at, 2), 2), :]

        group = [t for t in PARTNERS if t[1] == dy]
        send_plane(stat_of, r6s.at[q], 5, group)
        send_plane(num_of, r6.at[q], 4, group)
    own_at = 3 * 128 + (c * 4 + x) * 16
    r6[q] = numb[pl.ds(pl.multiple_of(own_at, 16), 16), :]
    r6s[q] = stat[pl.ds(pl.multiple_of(48 + (c * 4 + x) * 2, 2), 2), :]
    l_co.wait()
    await_plane(r6s, 5)
    stats = jnp.concatenate(
        [r6s[...].reshape(64, 128), jnp.zeros((64, 128), F32)], axis=0
    ).T
    lane8 = lax.broadcasted_iota(jnp.int32, (8, 128), 1)
    shares = []
    for r in range(2):
        valid = (lane8 < 64) & (lane8 % 2 == r)
        pair = []
        for h in range(2):
            peaks = jnp.where(valid, stats[h * 8 : (h + 1) * 8, :], NEG)
            totals = stats[16 + h * 8 : 16 + (h + 1) * 8, :]
            scale = jnp.where(valid, jnp.exp(peaks - jnp.max(peaks, axis=1, keepdims=True)), 0.0)
            pair.append((scale, jnp.sum(scale * totals, axis=1, keepdims=True)))
        shares.append(pair)
    await_plane(r6, 4)
    low = lane8 < 64
    for r in range(2):
        (scale0, total0), (scale1, total1) = shares[r]
        terms = []
        for s in range(PLANE):
            at = slice(2 * s + r, 2 * s + r + 1)
            scale = jnp.where(low, scale0[:, at], scale1[:, at])
            terms.append(r6[s].astype(F32)[r * 8 : (r + 1) * 8, :] * scale)
        row_f[r * 8 : (r + 1) * 8, :] = tree(terms) / jnp.where(low, total0, total1)
    final = (back(dot(two_rows(), co[...])) + middle).astype(BF16)
    hid[...] = final
    r7[p] = final

    for dx, dy, dc in PARTNERS:
        if dx == 0:
            pltpu.make_async_remote_copy(
                src_ref=hid,
                dst_ref=r7.at[p],
                send_sem=send_sem.at[6],
                recv_sem=recv_sem.at[6],
                device_id=(d, ys[dy] * 2 + cs[dc]),
                device_id_type=MESH,
            ).start()
    for n, ref in enumerate((r1, r2, r4, r5, r6, r6s)):
        await_bytes(ref.at[pl.ds(0, 31)], send_sem.at[n])
    await_bytes(r7.at[pl.ds(0, PATCH - 1)], recv_sem.at[6])
    hidf[...] = r7[...].astype(F32).reshape(128, 128)
    for j in range(CHUNKS):
        hidden_ref[:, j * 128 : (j + 1) * 128] = hidf[pl.ds(j, 16, stride=8), :].astype(BF16)
    await_bytes(r7.at[pl.ds(0, PATCH - 1)], send_sem.at[6])


def emit(hidden, new_k, new_v, hidden_ref, newk_ref, newv_ref):
    hidden_ref[...] = hidden[...]
    newk_ref[...] = new_k[...]
    newv_ref[...] = new_v[...]


def shards(
    token_ids,
    parents,
    embedding,
    self_gain,
    query_weight,
    key_weight,
    value_weight,
    output_weight,
    past_keys,
    past_values,
    cross_gain,
    cross_query,
    cross_output,
    image_keys,
    image_values,
):
    vmem = pl.BlockSpec(memory_space=pltpu.VMEM)
    hbm = pl.BlockSpec(memory_space=pl.ANY)
    shapes = ((16, D), (16, 128), (16, 128))
    results = pl.pallas_call(
        kernel,
        out_shape=tuple(pltpu.VMEM(shape, BF16) for shape in shapes),
        in_specs=[hbm] * 15,
        out_specs=(vmem, vmem, vmem),
        scratch_shapes=[
            pltpu.VMEM((4, 128), jnp.int32),
            pltpu.VMEM((4, 128), jnp.int32),
            pltpu.VMEM((8, 128), BF16),
            pltpu.VMEM((8, 128), BF16),
            pltpu.VMEM((1024, 128), BF16),
            pltpu.VMEM((D, 384), BF16),
            pltpu.VMEM((128, D), BF16),
            pltpu.VMEM((2048, 128), BF16),
            pltpu.VMEM((2048, 128), BF16),
            pltpu.VMEM((D, D), BF16),
            pltpu.VMEM((D, D), BF16),
            pltpu.VMEM((512, D), BF16),
            pltpu.VMEM((512, D), BF16),
            pltpu.VMEM((512, D), BF16),
            pltpu.VMEM((512, 128), BF16),
            pltpu.VMEM((DP, 16, 128), BF16),
            pltpu.VMEM((16, 128), BF16),
            pltpu.VMEM((PLANE, 16, 128), BF16),
            pltpu.VMEM((512, 128), F32),
            pltpu.VMEM((256, 128), BF16),
            pltpu.VMEM((512, 128), F32),
            pltpu.VMEM((512, 128), BF16),
            pltpu.VMEM((PLANE, 16, 128), BF16),
            pltpu.VMEM((64, 128), F32),
            pltpu.VMEM((16, 128), BF16),
            pltpu.VMEM((PLANE, 16, 128), BF16),
            pltpu.VMEM((512, 128), F32),
            pltpu.VMEM((512, 128), F32),
            pltpu.VMEM((512, 128), BF16),
            pltpu.VMEM((PLANE, 16, 128), BF16),
            pltpu.VMEM((ROWS, 128), F32),
            pltpu.VMEM((PLANE, 2, 128), F32),
            pltpu.VMEM((16, 128), BF16),
            pltpu.VMEM((PATCH, 16, 128), BF16),
            pltpu.VMEM((128, 128), F32),
            pltpu.SemaphoreType.DMA((15,)),
            pltpu.SemaphoreType.DMA((7,)),
            pltpu.SemaphoreType.DMA((7,)),
            pltpu.SemaphoreType.REGULAR((8,)),
        ],
        compiler_params=pltpu.CompilerParams(collective_id=0, has_side_effects=True),
        name="step",
    )(
        token_ids.reshape(4, 128),
        parents.reshape(4, 128),
        embedding,
        self_gain.reshape(8, 128),
        query_weight,
        key_weight,
        value_weight,
        output_weight,
        past_keys.reshape(2048, 128),
        past_values.reshape(2048, 128),
        cross_gain.reshape(8, 128),
        cross_query,
        cross_output,
        image_keys.reshape(512, D),
        image_values.reshape(512, D),
    )
    return pl.pallas_call(
        emit,
        out_shape=tuple(jax.ShapeDtypeStruct(shape, BF16) for shape in shapes),
        in_specs=[vmem] * 3,
        out_specs=(vmem, vmem, vmem),
        name="emit",
    )(*[pltpu.with_memory_space_constraint(r, pltpu.VMEM) for r in results])


def solution(mesh):
    in_specs = (
        P(),
        P(),
        P("dp", None),
        P(),
        P(None, "patch"),
        P(None, "patch"),
        P(None, "patch"),
        P("patch", None),
        P("dp", None, "patch"),
        P("dp", None, "patch"),
        P(),
        P(),
        P(),
        P("dp", None, "patch", None),
        P("dp", None, "patch", None),
    )
    out_specs = (P("dp", None), P("dp", "patch"), P("dp", "patch"))
    return jax.shard_map(
        shards, mesh=mesh, in_specs=in_specs, out_specs=out_specs, check_vma=False
    )
```

time: 58.1 us -> 52.1 us (0.90)
  local copies, waits for them, and re-layouts: 3.91 us -> 0 us
  Pallas kernels: 53.3 us -> 51.4 us
    unnamed x3 -> x0, local copies, waits for them, and re-layouts: 3.91 us -> none
    pallas_call x1 -> x2, Pallas kernels: 53.3 us -> 51.4 us  [the longest x1 50.8 us: shards(): pl.pallas_call(kernel, out_shape=tuple((pltpu.VMEM(shape, BF16) for shape...]
where the time goes in v2:
time: 52.1 us; the launch traced here: 52 us
  Pallas kernels  51.4 us (99%)
  between operations  0.64 us (1%)
    pallas_call x1, Pallas kernels, shards(): pl.pallas_call(kernel, out_shape=tuple((pltpu.VMEM(shape, BF16) for shape...  50.8 us

profile of v2, /device:TPU:1, one launch (start us, length us, event | category | flops | bytes accessed | tf_op | source)
XLA Modules:
  0.0 52.0 jit_solution(14371478450766019673)
XLA Ops:
  0.6 50.8 %step.1 = (bf16[16,1024]{1,0:T(8,128)(2,1)S(1)}, bf16[16,128]{1,0:T(8,128)(2,1)S(1)}, bf16[16,128]{1,0:T(8,128)(2,1)S(1)}) custom-call(s32[4,128]{1,0:T(4,128)} %bitcast.12, s32[4,128]{1,0:T(4,128)} %bitcast.13, bf16[1000,1024]{1,0:T(8,128)(2,1)} %emb_ref.1, bf16[8,128]{1,0:T(8,128)(2,1)} %bitcast.14, bf16[1024,128]{1,0:T(8,128)(2,1)} %wq_ref.1, ...), custom_call_target="tpu_custom_call" | custom-call | tf_op jit(solution)/shard_map/step/pallas_call | solution.py:468
  51.4 0.6 %emit.1 = (bf16[16,1024]{1,0:T(8,128)(2,1)}, bf16[16,128]{1,0:T(8,128)(2,1)}, bf16[16,128]{1,0:T(8,128)(2,1)}) custom-call(bf16[16,1024]{1,0:T(8,128)(2,1)S(1)} %get-tuple-element.6.hidden, bf16[16,128]{1,0:T(8,128)(2,1)S(1)} %get-tuple-element.7.new_k, bf16[16,128]{1,0:T(8,128)(2,1)S(1)} %get-tuple-element.8.new_v), custom_call_target="tpu_custom_call" | custom-call | tf_op jit(solution)/shard_map/emit/pallas_call | solution.py:533

commit v3 on v2

--- a/solution.py
+++ b/solution.py
@@ -122,6 +122,7 @@
     send_sem,
     recv_sem,
     ready,
+    in_plane,
 ):
     d = lax.axis_index("dp")
     p = lax.axis_index("patch")
@@ -150,15 +151,51 @@
     def signal(sem, device):
         pl.semaphore_signal(sem, inc=1, device_id=device, device_id_type=MESH)
 
-    for dz in range(1, 8):
-
-        @pl.when(z + dz < 8)
-        def _(dz=dz):
-            for dx in ACROSS:
-                signal(barrier, (zs[dz] * 4 + xs[dx], p))
-
-    for dx, dy, dc in PARTNERS:
-        signal(barrier, (z * 4 + xs[dx], ys[dy] * 2 + cs[dc]))
+    ps = [lax.rem(p + k, 8) for k in range(8)]
+
+    def later(of_z, of_plane):
+        for dz in range(1, 8):
+
+            @pl.when(z + dz < 8)
+            def _(dz=dz):
+                for dx in ACROSS:
+                    signal(of_z, (zs[dz] * 4 + xs[dx], p))
+
+        for dx in range(1, 4):
+
+            @pl.when(x + dx < 4)
+            def _(dx=dx):
+                for k in range(8):
+                    signal(of_plane, (z * 4 + xs[dx], ps[k]))
+
+        for k in range(1, 8):
+
+            @pl.when(p + k < 8)
+            def _(k=k):
+                signal(of_plane, (d, ps[k]))
+
+    def earlier(of_z, of_plane):
+        for dz in range(1, 8):
+
+            @pl.when(z + dz >= 8)
+            def _(dz=dz):
+                for dx in ACROSS:
+                    signal(of_z, (zs[dz] * 4 + xs[dx], p))
+
+        for dx in range(1, 4):
+
+            @pl.when(x + dx >= 4)
+            def _(dx=dx):
+                for k in range(8):
+                    signal(of_plane, (z * 4 + xs[dx], ps[k]))
+
+        for k in range(1, 8):
+
+            @pl.when(p + k >= 8)
+            def _(k=k):
+                signal(of_plane, (d, ps[k]))
+
+    later(barrier, barrier)
 
     l_q = load(wq_ref, wqkv.at[:, 0:128])
     l_k = load(wk_ref, wqkv.at[:, 128:256])
@@ -174,6 +211,12 @@
     l_iv = load(iv_ref, iv)
     l_co = load(co_ref, co)
 
+    @pl.when(4 * z + q > 0)
+    def _():
+        pl.semaphore_wait(barrier, 4 * z + q)
+
+    earlier(ready.at[z], in_plane)
+
     r256 = lax.broadcasted_iota(jnp.int32, (256, 128), 0)
     masks[...] = jnp.where(r256 // 16 == r256 % 16, 1.0, 0.0).astype(BF16)
     row_f[...] = jnp.zeros((64, 128), F32)
@@ -189,14 +232,6 @@
         rows = slice(n * 128, (n + 1) * 128)
         owned[rows, :] = dot(onehot[rows, :], emb[...]).astype(BF16)
 
-    pl.semaphore_wait(barrier, (PLANE - 1) + 4 * z)
-    for dz in range(1, 8):
-
-        @pl.when(z + dz >= 8)
-        def _(dz=dz):
-            for dx in ACROSS:
-                signal(ready.at[z], (zs[dz] * 4 + xs[dx], p))
-
     def await_bytes(ref, sem):
         pltpu.make_async_copy(ref, ref, sem).wait()
 
@@ -217,6 +252,11 @@
         def _(dz=dz):
             for dx in ACROSS:
                 send1(dz, dx)
+
+
+    @pl.when(q < PLANE - 1)
+    def _():
+        pl.semaphore_wait(in_plane, (PLANE - 1) - q)
 
     for dx in ACROSS[:3]:
         send1(0, dx)
@@ -510,6 +550,7 @@
             pltpu.SemaphoreType.DMA((7,)),
             pltpu.SemaphoreType.DMA((7,)),
             pltpu.SemaphoreType.REGULAR((8,)),
+            pltpu.SemaphoreType.REGULAR,
         ],
         compiler_params=pltpu.CompilerParams(collective_id=0, has_side_effects=True),
         name="step",

time: 52.1 us -> 52.7 us (1.012)
  Pallas kernels: 51.4 us -> 52 us
    pallas_call x1, Pallas kernels: 50.8 us -> 51.4 us  [shards(): pl.pallas_call(kernel, out_shape=tuple((pltpu.VMEM(shape, BF16) for shape...]
where the time goes in v3:
time: 52.7 us
  Pallas kernels  52 us (99%)
  between operations  0.64 us (1%)
    pallas_call x1, Pallas kernels, shards(): pl.pallas_call(kernel, out_shape=tuple((pltpu.VMEM(shape, BF16) for shape...  51.4 us

profile of v3, /device:TPU:1, one launch (start us, length us, event | category | flops | bytes accessed | tf_op | source)
XLA Modules:
  0.0 52.7 jit_solution(7307504921293134073)
XLA Ops:
  0.6 51.4 %step.1 = (bf16[16,1024]{1,0:T(8,128)(2,1)S(1)}, bf16[16,128]{1,0:T(8,128)(2,1)S(1)}, bf16[16,128]{1,0:T(8,128)(2,1)S(1)}) custom-call(s32[4,128]{1,0:T(4,128)} %bitcast.12, s32[4,128]{1,0:T(4,128)} %bitcast.13, bf16[1000,1024]{1,0:T(8,128)(2,1)} %emb_ref.1, bf16[8,128]{1,0:T(8,128)(2,1)} %bitcast.14, bf16[1024,128]{1,0:T(8,128)(2,1)} %wq_ref.1, ...), custom_call_target="tpu_custom_call" | custom-call | tf_op jit(solution)/shard_map/step/pallas_call | solution.py:508
  52.0 0.6 %emit.1 = (bf16[16,1024]{1,0:T(8,128)(2,1)}, bf16[16,128]{1,0:T(8,128)(2,1)}, bf16[16,128]{1,0:T(8,128)(2,1)}) custom-call(bf16[16,1024]{1,0:T(8,128)(2,1)S(1)} %get-tuple-element.6.hidden, bf16[16,128]{1,0:T(8,128)(2,1)S(1)} %get-tuple-element.7.new_k, bf16[16,128]{1,0:T(8,128)(2,1)S(1)} %get-tuple-element.8.new_v), custom_call_target="tpu_custom_call" | custom-call | tf_op jit(solution)/shard_map/emit/pallas_call | solution.py:574

commit v4 on v3

--- a/solution.py
+++ b/solution.py
@@ -102,7 +102,6 @@
     tokc,
     r2,
     tokf,
-    masks,
     part,
     partb,
     r4,
@@ -217,8 +216,6 @@
 
     earlier(ready.at[z], in_plane)
 
-    r256 = lax.broadcasted_iota(jnp.int32, (256, 128), 0)
-    masks[...] = jnp.where(r256 // 16 == r256 % 16, 1.0, 0.0).astype(BF16)
     row_f[...] = jnp.zeros((64, 128), F32)
 
     l_ids.wait()
@@ -274,8 +271,8 @@
     tokc[...] = chunk
     r2[q] = chunk
 
-    def send_plane(src_of, dst, n, partners=PARTNERS):
-        for dx, dy, dc in partners:
+    def send_plane(src_of, dst, n):
+        for dx, dy, dc in PARTNERS:
             to_x, to_p = xs[dx], ys[dy] * 2 + cs[dc]
             pltpu.make_async_remote_copy(
                 src_ref=src_of(to_x, to_p),
@@ -320,26 +317,30 @@
     newk_ref[...] = hidf[pl.ds(pl.multiple_of(x * 16, 16), 16), :].astype(BF16)
     newv_ref[...] = hidf[pl.ds(pl.multiple_of(ROWS + x * 16, 16), 16), :].astype(BF16)
 
-    mask_of = [masks[i * 16 : (i + 1) * 16, :] for i in range(IMAGES)]
-
-    def only(value, i):
-        return (value.reshape(8, 16, 128) * mask_of[i][None]).reshape(128, 128)
-
+    by_image = [pl.ds(i, 8, stride=16) for i in range(IMAGES)]
+    hidf[...] = queries.astype(F32)
     l_pk.wait()
-    scores = tree(
-        [dot_nt(only(queries, i), pk[i * LEN : (i + 1) * LEN, :]) for i in range(IMAGES)]
-    )
-    scores = scores * 0.125
+    parts = [
+        dot_nt(hidf[by_image[i], :].astype(BF16), pk[i * LEN : (i + 1) * LEN, :])
+        for i in range(IMAGES)
+    ]
+    for i in range(IMAGES):
+        hidf[by_image[i], :] = parts[i]
+    scores = hidf[...] * 0.125
     peak = jnp.maximum(jnp.max(scores, axis=1, keepdims=True), own)
     powers = jnp.exp(scores - peak)
     own_power = jnp.exp(own - peak)
     total = jnp.sum(powers, axis=1, keepdims=True) + own_power
-    weights = powers.astype(BF16)
     own_weight = own_power.astype(BF16).astype(F32)
+    hidf[...] = powers
     l_pv.wait()
-    context = tree(
-        [dot(only(weights, i), pv[i * LEN : (i + 1) * LEN, :]) for i in range(IMAGES)]
-    )
+    parts = [
+        dot(hidf[by_image[i], :].astype(BF16), pv[i * LEN : (i + 1) * LEN, :])
+        for i in range(IMAGES)
+    ]
+    for i in range(IMAGES):
+        hidf[by_image[i], :] = parts[i]
+    context = hidf[...]
     context = (context + own_weight * jnp.concatenate([new_v, new_v], axis=0)) / total
     context = join_heads(context)
     l_parents.wait()
@@ -390,46 +391,46 @@
     l_iv.wait()
     await_plane(r5, 3)
 
-    row32 = lax.broadcasted_iota(jnp.int32, (32, 128), 0)
-    image = (row32 // 8 % 2) * 2 + row32 % 2
-    same = image == lax.broadcasted_iota(jnp.int32, (32, 128), 1) // SPOTS
+    probf[...] = r5[...].astype(F32).reshape(512, 128)
+    units = [
+        (slice(g * 128, (g + 1) * 128), slice(j * 128, (j + 1) * 128), pl.ds(g * 128 + j, 16, stride=8))
+        for g in range(4)
+        for j in range(CHUNKS)
+    ]
+    scores = jnp.concatenate(
+        [dot_nt(split_heads(probf[rows, :]), ik[keys, block]) for keys, block, rows in units], axis=0
+    )
+    row = lax.broadcasted_iota(jnp.int32, scores.shape, 0)
+    image = (row // 8 % 2) * 2 + row % 2
+    same = image == lax.broadcasted_iota(jnp.int32, scores.shape, 1) // SPOTS
+    scores = jnp.where(same, scores * 0.125, NEG)
+    peak = jnp.max(scores, axis=1, keepdims=True)
+    powers = jnp.exp(scores - peak)
+    total = jnp.sum(powers, axis=1, keepdims=True)
+    powers = powers.astype(BF16)
     lane = lax.broadcasted_iota(jnp.int32, (16, 128), 1)
-    for g, dy in enumerate(ACROSS):
-        base = pl.multiple_of(ys[dy] * 128, 128)
-        here = slice(g * 128, (g + 1) * 128)
-        probf[here, :] = r5[pl.ds(ys[dy] * 8, 8)].astype(F32).reshape(128, 128)
+    for g in range(4):
         stats = jnp.zeros((16, 128), F32)
         for j in range(CHUNKS):
-            block = slice(j * 128, (j + 1) * 128)
-            probes = split_heads(probf[pl.ds(g * 128 + j, 16, stride=8), :])
-            scores = dot_nt(probes, ik[pl.ds(base, 128), block]) * 0.125
-            scores = jnp.where(same, scores, NEG)
-            peak = jnp.max(scores, axis=1, keepdims=True)
-            powers = jnp.exp(scores - peak)
-            total = jnp.sum(powers, axis=1, keepdims=True)
-            summed = join_heads(dot(powers.astype(BF16), iv[pl.ds(base, 128), block]))
-            num[pl.ds(g * 128 + j, 16, stride=8), :] = summed
             for h in range(2):
-                rows = slice(h * 16, (h + 1) * 16)
-                stats = jnp.where(lane == h * 8 + j, peak[rows], stats)
-                stats = jnp.where(lane == 16 + h * 8 + j, total[rows], stats)
+                at = (g * CHUNKS + j) * 32 + h * 16
+                stats = jnp.where(lane == h * 8 + j, peak[at : at + 16], stats)
+                stats = jnp.where(lane == 16 + h * 8 + j, total[at : at + 16], stats)
         stat[g * 16 : (g + 1) * 16, :] = stats
-        numb[here, :] = num[here, :].astype(BF16)
-
-        def num_of(to_x, to_p, g=g):
-            at = g * 128 + ((to_p % 2) * 4 + to_x) * 16
-            return numb.at[pl.ds(pl.multiple_of(at, 16), 16), :]
-
-        def stat_of(to_x, to_p, g=g):
-            at = g * 16 + ((to_p % 2) * 4 + to_x) * 2
-            return stat.at[pl.ds(pl.multiple_of(at, 2), 2), :]
-
-        group = [t for t in PARTNERS if t[1] == dy]
-        send_plane(stat_of, r6s.at[q], 5, group)
-        send_plane(num_of, r6.at[q], 4, group)
-    own_at = 3 * 128 + (c * 4 + x) * 16
-    r6[q] = numb[pl.ds(pl.multiple_of(own_at, 16), 16), :]
-    r6s[q] = stat[pl.ds(pl.multiple_of(48 + (c * 4 + x) * 2, 2), 2), :]
+    for n, (keys, block, rows) in enumerate(units):
+        num[rows, :] = join_heads(dot(powers[n * 32 : (n + 1) * 32], iv[keys, block]))
+    numb[...] = num[...].astype(BF16)
+
+    def num_of(to_x, to_p):
+        return numb.at[pl.ds(pl.multiple_of((to_p * 4 + to_x) * 16, 16), 16), :]
+
+    def stat_of(to_x, to_p):
+        return stat.at[pl.ds(pl.multiple_of((to_p * 4 + to_x) * 2, 2), 2), :]
+
+    send_plane(stat_of, r6s.at[q], 5)
+    send_plane(num_of, r6.at[q], 4)
+    r6[q] = numb[pl.ds(pl.multiple_of(slot * 16, 16), 16), :]
+    r6s[q] = stat[pl.ds(pl.multiple_of(slot * 2, 2), 2), :]
     l_co.wait()
     await_plane(r6s, 5)
     stats = jnp.concatenate(
@@ -530,7 +531,6 @@
             pltpu.VMEM((16, 128), BF16),
             pltpu.VMEM((PLANE, 16, 128), BF16),
             pltpu.VMEM((512, 128), F32),
-            pltpu.VMEM((256, 128), BF16),
             pltpu.VMEM((512, 128), F32),
             pltpu.VMEM((512, 128), BF16),
             pltpu.VMEM((PLANE, 16, 128), BF16),

time: 52.7 us -> 46.4 us (0.88)
  Pallas kernels: 52 us -> 45.7 us
    pallas_call x1, Pallas kernels: 51.4 us -> 45 us  [shards(): pl.pallas_call(kernel, out_shape=tuple((pltpu.VMEM(shape, BF16) for shape...]
where the time goes in v4:
time: 46.4 us; the launch traced here: 46.3 us
  Pallas kernels  45.7 us (98%)
  between operations  0.64 us (1%)
    pallas_call x1, Pallas kernels, shards(): pl.pallas_call(kernel, out_shape=tuple((pltpu.VMEM(shape, BF16) for shape...  45 us

profile of v4, /device:TPU:1, one launch (start us, length us, event | category | flops | bytes accessed | tf_op | source)
XLA Modules:
  0.0 46.3 jit_solution(1721902049124073316)
XLA Ops:
  0.6 45.0 %step.1 = (bf16[16,1024]{1,0:T(8,128)(2,1)S(1)}, bf16[16,128]{1,0:T(8,128)(2,1)S(1)}, bf16[16,128]{1,0:T(8,128)(2,1)S(1)}) custom-call(s32[4,128]{1,0:T(4,128)} %bitcast.12, s32[4,128]{1,0:T(4,128)} %bitcast.13, bf16[1000,1024]{1,0:T(8,128)(2,1)} %emb_ref.1, bf16[8,128]{1,0:T(8,128)(2,1)} %bitcast.14, bf16[1024,128]{1,0:T(8,128)(2,1)} %wq_ref.1, ...), custom_call_target="tpu_custom_call" | custom-call | tf_op jit(solution)/shard_map/step/pallas_call | solution.py:509
  45.7 0.6 %emit.1 = (bf16[16,1024]{1,0:T(8,128)(2,1)}, bf16[16,128]{1,0:T(8,128)(2,1)}, bf16[16,128]{1,0:T(8,128)(2,1)}) custom-call(bf16[16,1024]{1,0:T(8,128)(2,1)S(1)} %get-tuple-element.6.hidden, bf16[16,128]{1,0:T(8,128)(2,1)S(1)} %get-tuple-element.7.new_k, bf16[16,128]{1,0:T(8,128)(2,1)S(1)} %get-tuple-element.8.new_v), custom_call_target="tpu_custom_call" | custom-call | tf_op jit(solution)/shard_map/emit/pallas_call | solution.py:574

commit v5 on v4

--- a/solution.py
+++ b/solution.py
@@ -121,7 +121,6 @@
     send_sem,
     recv_sem,
     ready,
-    in_plane,
 ):
     d = lax.axis_index("dp")
     p = lax.axis_index("patch")
@@ -150,51 +149,15 @@
     def signal(sem, device):
         pl.semaphore_signal(sem, inc=1, device_id=device, device_id_type=MESH)
 
-    ps = [lax.rem(p + k, 8) for k in range(8)]
-
-    def later(of_z, of_plane):
-        for dz in range(1, 8):
-
-            @pl.when(z + dz < 8)
-            def _(dz=dz):
-                for dx in ACROSS:
-                    signal(of_z, (zs[dz] * 4 + xs[dx], p))
-
-        for dx in range(1, 4):
-
-            @pl.when(x + dx < 4)
-            def _(dx=dx):
-                for k in range(8):
-                    signal(of_plane, (z * 4 + xs[dx], ps[k]))
-
-        for k in range(1, 8):
-
-            @pl.when(p + k < 8)
-            def _(k=k):
-                signal(of_plane, (d, ps[k]))
-
-    def earlier(of_z, of_plane):
-        for dz in range(1, 8):
-
-            @pl.when(z + dz >= 8)
-            def _(dz=dz):
-                for dx in ACROSS:
-                    signal(of_z, (zs[dz] * 4 + xs[dx], p))
-
-        for dx in range(1, 4):
-
-            @pl.when(x + dx >= 4)
-            def _(dx=dx):
-                for k in range(8):
-                    signal(of_plane, (z * 4 + xs[dx], ps[k]))
-
-        for k in range(1, 8):
-
-            @pl.when(p + k >= 8)
-            def _(k=k):
-                signal(of_plane, (d, ps[k]))
-
-    later(barrier, barrier)
+    for dz in range(1, 8):
+
+        @pl.when(z + dz < 8)
+        def _(dz=dz):
+            for dx in ACROSS:
+                signal(barrier, (zs[dz] * 4 + xs[dx], p))
+
+    for dx, dy, dc in PARTNERS:
+        signal(barrier, (z * 4 + xs[dx], ys[dy] * 2 + cs[dc]))
 
     l_q = load(wq_ref, wqkv.at[:, 0:128])
     l_k = load(wk_ref, wqkv.at[:, 128:256])
@@ -210,12 +173,6 @@
     l_iv = load(iv_ref, iv)
     l_co = load(co_ref, co)
 
-    @pl.when(4 * z + q > 0)
-    def _():
-        pl.semaphore_wait(barrier, 4 * z + q)
-
-    earlier(ready.at[z], in_plane)
-
     row_f[...] = jnp.zeros((64, 128), F32)
 
     l_ids.wait()
@@ -229,6 +186,14 @@
         rows = slice(n * 128, (n + 1) * 128)
         owned[rows, :] = dot(onehot[rows, :], emb[...]).astype(BF16)
 
+    pl.semaphore_wait(barrier, (PLANE - 1) + 4 * z)
+    for dz in range(1, 8):
+
+        @pl.when(z + dz >= 8)
+        def _(dz=dz):
+            for dx in ACROSS:
+                signal(ready.at[z], (zs[dz] * 4 + xs[dx], p))
+
     def await_bytes(ref, sem):
         pltpu.make_async_copy(ref, ref, sem).wait()
 
@@ -249,11 +214,6 @@
         def _(dz=dz):
             for dx in ACROSS:
                 send1(dz, dx)
-
-
-    @pl.when(q < PLANE - 1)
-    def _():
-        pl.semaphore_wait(in_plane, (PLANE - 1) - q)
 
     for dx in ACROSS[:3]:
         send1(0, dx)
@@ -550,7 +510,6 @@
             pltpu.SemaphoreType.DMA((7,)),
             pltpu.SemaphoreType.DMA((7,)),
             pltpu.SemaphoreType.REGULAR((8,)),
-            pltpu.SemaphoreType.REGULAR,
         ],
         compiler_params=pltpu.CompilerParams(collective_id=0, has_side_effects=True),
         name="step",

time: 46.4 us -> 45.7 us (0.985)
  Pallas kernels: 45.7 us -> 45 us
    pallas_call x1, Pallas kernels: 45 us -> 44.3 us  [shards(): pl.pallas_call(kernel, out_shape=tuple((pltpu.VMEM(shape, BF16) for shape...]
where the time goes in v5:
time: 45.7 us; the launch traced here: 45.6 us
  Pallas kernels  45 us (98%)
  between operations  0.64 us (1%)
    pallas_call x1, Pallas kernels, shards(): pl.pallas_call(kernel, out_shape=tuple((pltpu.VMEM(shape, BF16) for shape...  44.3 us

profile of v5, /device:TPU:1, one launch (start us, length us, event | category | flops | bytes accessed | tf_op | source)
XLA Modules:
  0.0 45.6 jit_solution(17282226702915039861)
XLA Ops:
  0.6 44.3 %step.1 = (bf16[16,1024]{1,0:T(8,128)(2,1)S(1)}, bf16[16,128]{1,0:T(8,128)(2,1)S(1)}, bf16[16,128]{1,0:T(8,128)(2,1)S(1)}) custom-call(s32[4,128]{1,0:T(4,128)} %bitcast.12, s32[4,128]{1,0:T(4,128)} %bitcast.13, bf16[1000,1024]{1,0:T(8,128)(2,1)} %emb_ref.1, bf16[8,128]{1,0:T(8,128)(2,1)} %bitcast.14, bf16[1024,128]{1,0:T(8,128)(2,1)} %wq_ref.1, ...), custom_call_target="tpu_custom_call" | custom-call | tf_op jit(solution)/shard_map/step/pallas_call | solution.py:469
  45.0 0.6 %emit.1 = (bf16[16,1024]{1,0:T(8,128)(2,1)}, bf16[16,128]{1,0:T(8,128)(2,1)}, bf16[16,128]{1,0:T(8,128)(2,1)}) custom-call(bf16[16,1024]{1,0:T(8,128)(2,1)S(1)} %get-tuple-element.6.hidden, bf16[16,128]{1,0:T(8,128)(2,1)S(1)} %get-tuple-element.7.new_k, bf16[16,128]{1,0:T(8,128)(2,1)S(1)} %get-tuple-element.8.new_v), custom_call_target="tpu_custom_call" | custom-call | tf_op jit(solution)/shard_map/emit/pallas_call | solution.py:533

commit v6 on v5

--- a/solution.py
+++ b/solution.py
@@ -257,8 +257,6 @@
         jnp.concatenate([r2[b * 8 + j] for b in range(BEAMS)], axis=0).astype(F32)
         for j in range(CHUNKS)
     ]
-    for j in range(CHUNKS):
-        tokf[pl.ds(j, ROWS, stride=8), :] = toks[j]
     square = tree([t * t for t in toks])
     factor = lax.rsqrt(jnp.sum(square, axis=1, keepdims=True) * (1.0 / D) + 1e-06)
     sgain = sgain_ref[...].astype(F32)
@@ -272,10 +270,6 @@
         queries.astype(F32) * jnp.concatenate([new_k, new_k], axis=0), axis=1, keepdims=True
     )
     own = own * 0.125
-    hidf[0:ROWS, :] = new_k
-    hidf[ROWS : 2 * ROWS, :] = new_v
-    newk_ref[...] = hidf[pl.ds(pl.multiple_of(x * 16, 16), 16), :].astype(BF16)
-    newv_ref[...] = hidf[pl.ds(pl.multiple_of(ROWS + x * 16, 16), 16), :].astype(BF16)
 
     by_image = [pl.ds(i, 8, stride=16) for i in range(IMAGES)]
     hidf[...] = queries.astype(F32)
@@ -320,10 +314,16 @@
 
     send_plane(part_of, r4.at[q], 2)
     r4[q] = partb[mine, :]
+    hidf[0:ROWS, :] = new_k
+    hidf[ROWS : 2 * ROWS, :] = new_v
+    newk_ref[...] = hidf[pl.ds(pl.multiple_of(x * 16, 16), 16), :].astype(BF16)
+    newv_ref[...] = hidf[pl.ds(pl.multiple_of(ROWS + x * 16, 16), 16), :].astype(BF16)
+    for j in range(CHUNKS):
+        tokf[pl.ds(j, 16, stride=8), :] = r2[x * 8 + j].astype(F32)
     l_cgain.wait()
     l_cq.wait()
     await_plane(r4, 2)
-    middle = tree([r4[s].astype(F32) for s in range(PLANE)]) + tokf[mine, :]
+    middle = tree([r4[s].astype(F32) for s in range(PLANE)]) + tokf[pl.ds(pl.multiple_of(p * 16, 16), 16), :]
 
     cgain = cgain_ref[...].astype(F32)
     for r in range(2):
@@ -377,6 +377,10 @@
                 stats = jnp.where(lane == h * 8 + j, peak[at : at + 16], stats)
                 stats = jnp.where(lane == 16 + h * 8 + j, total[at : at + 16], stats)
         stat[g * 16 : (g + 1) * 16, :] = stats
+    def stat_of(to_x, to_p):
+        return stat.at[pl.ds(pl.multiple_of((to_p * 4 + to_x) * 2, 2), 2), :]
+
+    send_plane(stat_of, r6s.at[q], 5)
     for n, (keys, block, rows) in enumerate(units):
         num[rows, :] = join_heads(dot(powers[n * 32 : (n + 1) * 32], iv[keys, block]))
     numb[...] = num[...].astype(BF16)
@@ -384,10 +388,6 @@
     def num_of(to_x, to_p):
         return numb.at[pl.ds(pl.multiple_of((to_p * 4 + to_x) * 16, 16), 16), :]
 
-    def stat_of(to_x, to_p):
-        return stat.at[pl.ds(pl.multiple_of((to_p * 4 + to_x) * 2, 2), 2), :]
-
-    send_plane(stat_of, r6s.at[q], 5)
     send_plane(num_of, r6.at[q], 4)
     r6[q] = numb[pl.ds(pl.multiple_of(slot * 16, 16), 16), :]
     r6s[q] = stat[pl.ds(pl.multiple_of(slot * 2, 2), 2), :]
@@ -490,7 +490,7 @@
             pltpu.VMEM((DP, 16, 128), BF16),
             pltpu.VMEM((16, 128), BF16),
             pltpu.VMEM((PLANE, 16, 128), BF16),
-            pltpu.VMEM((512, 128), F32),
+            pltpu.VMEM((128, 128), F32),
             pltpu.VMEM((512, 128), F32),
             pltpu.VMEM((512, 128), BF16),
             pltpu.VMEM((PLANE, 16, 128), BF16),

time: 45.7 us -> 45.9 us (level)
  no operation moved by 1% of the time
where the time goes in v6:
time: 45.9 us; the launch traced here: 45.8 us
  Pallas kernels  45.1 us (98%)
  between operations  0.64 us (1%)
    pallas_call x1, Pallas kernels, shards(): pl.pallas_call(kernel, out_shape=tuple((pltpu.VMEM(shape, BF16) for shape...  44.5 us

profile of v6, /device:TPU:1, one launch (start us, length us, event | category | flops | bytes accessed | tf_op | source)
XLA Modules:
  0.0 45.8 jit_solution(18302252158882246642)
XLA Ops:
  0.6 44.5 %step.1 = (bf16[16,1024]{1,0:T(8,128)(2,1)S(1)}, bf16[16,128]{1,0:T(8,128)(2,1)S(1)}, bf16[16,128]{1,0:T(8,128)(2,1)S(1)}) custom-call(s32[4,128]{1,0:T(4,128)} %bitcast.12, s32[4,128]{1,0:T(4,128)} %bitcast.13, bf16[1000,1024]{1,0:T(8,128)(2,1)} %emb_ref.1, bf16[8,128]{1,0:T(8,128)(2,1)} %bitcast.14, bf16[1024,128]{1,0:T(8,128)(2,1)} %wq_ref.1, ...), custom_call_target="tpu_custom_call" | custom-call | tf_op jit(solution)/shard_map/step/pallas_call | solution.py:469
  45.1 0.6 %emit.1 = (bf16[16,1024]{1,0:T(8,128)(2,1)}, bf16[16,128]{1,0:T(8,128)(2,1)}, bf16[16,128]{1,0:T(8,128)(2,1)}) custom-call(bf16[16,1024]{1,0:T(8,128)(2,1)S(1)} %get-tuple-element.6.hidden, bf16[16,128]{1,0:T(8,128)(2,1)S(1)} %get-tuple-element.7.new_k, bf16[16,128]{1,0:T(8,128)(2,1)S(1)} %get-tuple-element.8.new_v), custom_call_target="tpu_custom_call" | custom-call | tf_op jit(solution)/shard_map/emit/pallas_call | solution.py:533

commit v7 on v6

--- a/solution.py
+++ b/solution.py
@@ -159,6 +159,15 @@
     for dx, dy, dc in PARTNERS:
         signal(barrier, (z * 4 + xs[dx], ys[dy] * 2 + cs[dc]))
 
+    row_f[...] = jnp.zeros((64, 128), F32)
+
+    l_ids.wait()
+    lane1024 = lax.broadcasted_iota(jnp.int32, (128, 1024), 1)
+    for n in range(4):
+        col = jnp.broadcast_to(ids_ref[n : n + 1, :], (128, 128)).T - d * SLAB
+        wide = jnp.concatenate([col] * 8, axis=1)
+        onehot[n * 128 : (n + 1) * 128, :] = jnp.where(wide == lane1024, 1.0, 0.0).astype(BF16)
+    l_emb.wait()
     l_q = load(wq_ref, wqkv.at[:, 0:128])
     l_k = load(wk_ref, wqkv.at[:, 128:256])
     l_v = load(wv_ref, wqkv.at[:, 256:384])
@@ -172,16 +181,6 @@
     l_ik = load(ik_ref, ik)
     l_iv = load(iv_ref, iv)
     l_co = load(co_ref, co)
-
-    row_f[...] = jnp.zeros((64, 128), F32)
-
-    l_ids.wait()
-    lane1024 = lax.broadcasted_iota(jnp.int32, (128, 1024), 1)
-    for n in range(4):
-        col = jnp.broadcast_to(ids_ref[n : n + 1, :], (128, 128)).T - d * SLAB
-        wide = jnp.concatenate([col] * 8, axis=1)
-        onehot[n * 128 : (n + 1) * 128, :] = jnp.where(wide == lane1024, 1.0, 0.0).astype(BF16)
-    l_emb.wait()
     for n in range(4):
         rows = slice(n * 128, (n + 1) * 128)
         owned[rows, :] = dot(onehot[rows, :], emb[...]).astype(BF16)

time: 45.9 us -> 45.9 us (level)
  no operation moved by 1% of the time
where the time goes in v7:
time: 45.9 us; the launch traced here: 45.8 us
  Pallas kernels  45.1 us (98%)
  between operations  0.64 us (1%)
    pallas_call x1, Pallas kernels, shards(): pl.pallas_call(kernel, out_shape=tuple((pltpu.VMEM(shape, BF16) for shape...  44.5 us

profile of v7, /device:TPU:1, one launch (start us, length us, event | category | flops | bytes accessed | tf_op | source)
XLA Modules:
  0.0 45.8 jit_solution(14362015770929890156)
XLA Ops:
  0.6 44.5 %step.1 = (bf16[16,1024]{1,0:T(8,128)(2,1)S(1)}, bf16[16,128]{1,0:T(8,128)(2,1)S(1)}, bf16[16,128]{1,0:T(8,128)(2,1)S(1)}) custom-call(s32[4,128]{1,0:T(4,128)} %bitcast.12, s32[4,128]{1,0:T(4,128)} %bitcast.13, bf16[1000,1024]{1,0:T(8,128)(2,1)} %emb_ref.1, bf16[8,128]{1,0:T(8,128)(2,1)} %bitcast.14, bf16[1024,128]{1,0:T(8,128)(2,1)} %wq_ref.1, ...), custom_call_target="tpu_custom_call" | custom-call | tf_op jit(solution)/shard_map/step/pallas_call | solution.py:468
  45.1 0.6 %emit.1 = (bf16[16,1024]{1,0:T(8,128)(2,1)}, bf16[16,128]{1,0:T(8,128)(2,1)}, bf16[16,128]{1,0:T(8,128)(2,1)}) custom-call(bf16[16,1024]{1,0:T(8,128)(2,1)S(1)} %get-tuple-element.6.hidden, bf16[16,128]{1,0:T(8,128)(2,1)S(1)} %get-tuple-element.7.new_k, bf16[16,128]{1,0:T(8,128)(2,1)S(1)} %get-tuple-element.8.new_v), custom_call_target="tpu_custom_call" | custom-call | tf_op jit(solution)/shard_map/emit/pallas_call | solution.py:532
